TPU v7x, 32 devices: a whole 2x2x4 slice. The times are simulated.
32 devices in a mesh: groups: 2 (over y), curve: 16 (over z, x, core).
Axes of the slice: x: 2, y: 2, z: 4, core: 2. Of those that a mesh axis runs over, the one named last changes fastest.
Arguments:
- tracer_mass: float32 [9216, 200], P(('groups', 'curve')), parts along dimension 0, may hold values from 0.1 to 10
- send_ids: int32 [128, 32], P(('groups', 'curve')), parts along dimension 0, may hold values from 0 to 31, as said below
- send_counts: int32 [128], P(('groups', 'curve')), parts along dimension 0, may hold values from 1 to 32, as said below
- sources: int32 [9216, 4], P(('groups', 'curve')), parts along dimension 0, may hold values from 0 to 1439
- fractions: float32 [9216, 4], P(('groups', 'curve')), parts along dimension 0, may hold values from 0.02 to 0.25
- moments: float32 [2, 9216, 4], P(None, ('groups', 'curve')), parts along dimension 1, may hold values from -0.5 to 0.5
Outputs:
- new_mass: float32 [9216, 200], P(('groups', 'curve')), parts along dimension 0
There are 2 independent parts, one for each index of `groups`. A program takes and returns all parts, laid end to end along the dimension named above; each array names one. Nothing has to cross between parts.
Inputs may be any that keep to these rules, and one draw needn't show every extreme that they name: `send_ids`: each row holds distinct local element indices of the owning device. `send_counts`: slots below the count are live; in every draw some lists reach 32. `sources`: indices into the device's own extended cells.
All inputs are finite; a program needn't handle non-finite values.
Results may differ from a plain program's by a relative error of at most 0.0001.
Values sent between devices are 32-bit elements; how exact they have to be, the bound alone decides.
No kernel may reach another device: no remote copies, remote signals or barrier semaphores. Data moves between devices by JAX's collectives and lax.ppermute only.
A program may use at most 64 MiB of HBM per device.

v0:
```python
import jax
import jax.numpy as jnp
from jax import lax
from jax.sharding import PartitionSpec as P

OFFSETS = (1, 2, -1, -2)


def from_behind(x, axis, by):
    count = lax.axis_size(axis)
    return lax.ppermute(x, axis, [(i, (i + by) % count) for i in range(count)])


def build_slopes(values):
    count = values.shape[0]
    index = jnp.arange(count, dtype=jnp.int32)
    column = (index % 3)[:, None]
    row_pos = (index // 3 % 3)[:, None]
    right = jnp.roll(values, -1, axis=0)
    left = jnp.roll(values, 1, axis=0)
    below = jnp.roll(values, -3, axis=0)
    above = jnp.roll(values, 3, axis=0)
    slope_x = jnp.where(
        column == 0, right - values, jnp.where(column == 1, 0.5 * (right - left), values - left)
    )
    slope_y = jnp.where(
        row_pos == 0, below - values, jnp.where(row_pos == 1, 0.5 * (below - above), values - above)
    )
    return (slope_x, slope_y)


def transport(extended, sources_dev, fraction_dev, moment_x, moment_y):
    width = extended.shape[-1]
    total_cells = extended.shape[0]
    slope_x, slope_y = build_slopes(extended)
    inflow = jnp.zeros((sources_dev.shape[0], width), jnp.float32)
    outflow = jnp.zeros((total_cells, width), jnp.float32)
    for column in range(sources_dev.shape[1]):
        source = sources_dev[:, column]
        flux = fraction_dev[:, column, None] * (
            extended[source]
            + moment_x[:, column, None] * slope_x[source]
            + moment_y[:, column, None] * slope_y[source]
        )
        inflow = inflow + flux
        outflow = outflow + jax.ops.segment_sum(flux, source, num_segments=total_cells)
    return (inflow, outflow)


def local(tracer_mass, send_ids, send_counts, sources, fractions, moments):
    own_cells = tracer_mass.shape[0]
    width = tracer_mass.shape[1]
    slots = send_ids.shape[1]
    list_cells = 9 * slots
    live = (jnp.arange(slots, dtype=jnp.int32)[None, :] < send_counts[:, None]).astype(jnp.float32)
    cell_ids = (9 * send_ids[:, :, None] + jnp.arange(9, dtype=jnp.int32)[None, None, :]).reshape(
        4, list_cells
    )
    live_cells = (live[:, :, None] * jnp.ones((1, 1, 9), jnp.float32)).reshape(4, list_cells)
    packed = tracer_mass[cell_ids] * live_cells[..., None]
    received = jnp.stack([from_behind(packed[slot], "curve", OFFSETS[slot]) for slot in range(4)])
    extended = jnp.concatenate([tracer_mass, received.reshape(4 * list_cells, width)], axis=0)
    inflow, outflow = transport(extended, sources, fractions, moments[0], moments[1])
    owned = outflow[:own_cells]
    returned = outflow[own_cells:].reshape(4, list_cells, width)
    back = jnp.stack([from_behind(returned[slot], "curve", -OFFSETS[slot]) for slot in range(4)])
    back = back * live_cells[..., None]
    owned = owned.at[cell_ids.reshape(-1)].add(back.reshape(-1, width))
    return tracer_mass + inflow - owned


def solution(mesh):
    placed = (
        P(("groups", "curve"), None),
        P(("groups", "curve"), None),
        P(("groups", "curve")),
        P(("groups", "curve"), None),
        P(("groups", "curve"), None),
        P(None, ("groups", "curve"), None),
    )
    return jax.shard_map(
        local, mesh=mesh, in_specs=placed, out_specs=P(("groups", "curve"), None), check_vma=False
    )
```

profile of v0, /device:TPU:5, one launch (start us, length us, event | category | flops | bytes accessed | tf_op | source)
XLA Modules:
  0.0 110.3 jit_solution(11244870543557881163)
XLA Ops:
  2.1 3.3 %gather_fusion = f32[1152,200]{1,0:T(8,128)S(1)} fusion(f32[288,200]{1,0:T(8,128)S(1)} %copy-done, s32[2048]{0:T(1024)S(1)} %pad_clamp_fusion), kind=kCustom, calls=%fused_computation | custom fusion | bytes 1847808 | tf_op jit(solution)/shard_map/gather | solution.py:60
  7.5 3.0 %collective-permute-start.3 = (f32[288,200]{1,0:T(8,128)S(1)}, f32[288,200]{1,0:T(8,128)S(1)}, u32[]{:S(2)}, u32[]{:S(2)}) collective-permute-start(f32[288,200]{1,0:T(8,128)S(1)} %get-tuple-element.34), channel_id=1, source_target_pairs={{0,14},{1,15},{2,0},{3,1},{4,2},{5,3},{6,4},{7,5},{8,6},{9,7},{10,... | collective-permute-start | bytes 691208 | tf_op jit(solution)/shard_map/ppermute | solution.py:11
  13.9 8.3 %collective-permute-done = f32[288,200]{1,0:T(8,128)S(1)} collective-permute-done((f32[288,200]{1,0:T(8,128)S(1)}, f32[288,200]{1,0:T(8,128)S(1)}, u32[]{:S(2)}, u32[]{:S(2)}) %collective-permute-start) | collective-permute-done | bytes 230432 | tf_op jit(solution)/shard_map/ppermute | solution.py:11
  22.2 3.5 %collective-permute-done.3 = f32[288,200]{1,0:T(8,128)S(1)} collective-permute-done((f32[288,200]{1,0:T(8,128)S(1)}, f32[288,200]{1,0:T(8,128)S(1)}, u32[]{:S(2)}, u32[]{:S(2)}) %collective-permute-start.3) | collective-permute-done | bytes 230432 | tf_op jit(solution)/shard_map/ppermute | solution.py:11
  25.8 2.6 %collective-permute-done.2 = f32[288,200]{1,0:T(8,128)S(1)} collective-permute-done((f32[288,200]{1,0:T(8,128)S(1)}, f32[288,200]{1,0:T(8,128)S(1)}, u32[]{:S(2)}, u32[]{:S(2)}) %collective-permute-start.2) | collective-permute-done | bytes 230432 | tf_op jit(solution)/shard_map/ppermute | solution.py:11
  29.4 4.1 %select_select_fusion.1 = (f32[1440,200]{1,0:T(8,128)}, f32[1440,200]{1,0:T(8,128)S(1)}, f32[1440,200]{1,0:T(8,128)S(1)}) fusion(f32[1439,200]{1,0:T(8,128)S(1)} %get-tuple-element.30, f32[1,200]{1,0:T(1,128)S(1)} %slice.194, f32[1,200]{1,0:T(1,128)S(1)} %slice-done, f32[1439,200]{1,0:T(8,128)S(1)} %get-tuple-element.29, ...), kind=kLoop, calls=%fused_computation.33 | loop fusion | flops 4896000 | bytes 9221760 | tf_op jit(solution)/shard_map/jit(_where)/select_n | solution.py:23
  33.6 3.5 %gather_fusion.11 = f32[288,200]{1,0:T(8,128)} fusion(f32[1440,200]{1,0:T(8,128)} %get-tuple-element.26, s32[1024]{0:T(1024)S(1)} %get-tuple-element.43), kind=kCustom, calls=%fused_computation.11 | custom fusion | bytes 461952 | tf_op jit(solution)/shard_map/gather | solution.py:42
  37.1 3.5 %gather_fusion.8 = f32[288,200]{1,0:T(8,128)} fusion(f32[1440,200]{1,0:T(8,128)} %get-tuple-element.26, s32[1024]{0:T(1024)S(1)} %get-tuple-element.44), kind=kCustom, calls=%fused_computation.8 | custom fusion | bytes 461952 | tf_op jit(solution)/shard_map/gather | solution.py:42
  40.6 2.1 %gather_fusion.12 = f32[288,200]{1,0:T(8,128)} fusion(f32[1440,200]{1,0:T(8,128)S(1)} %get-tuple-element.27, s32[1024]{0:T(1024)S(1)} %get-tuple-element.43), kind=kCustom, calls=%fused_computation.12 | custom fusion | bytes 461952 | tf_op jit(solution)/shard_map/gather | solution.py:43
  42.7 2.1 %gather_fusion.9 = f32[288,200]{1,0:T(8,128)} fusion(f32[1440,200]{1,0:T(8,128)S(1)} %get-tuple-element.27, s32[1024]{0:T(1024)S(1)} %get-tuple-element.44), kind=kCustom, calls=%fused_computation.9 | custom fusion | bytes 461952 | tf_op jit(solution)/shard_map/gather | solution.py:43
  44.8 2.1 %gather_fusion.10 = f32[288,200]{1,0:T(8,128)} fusion(f32[1440,200]{1,0:T(8,128)S(1)} %get-tuple-element.28, s32[1024]{0:T(1024)S(1)} %get-tuple-element.43), kind=kCustom, calls=%fused_computation.10 | custom fusion | bytes 461952 | tf_op jit(solution)/shard_map/gather | solution.py:41
  47.0 2.1 %gather_fusion.7 = f32[288,200]{1,0:T(8,128)} fusion(f32[1440,200]{1,0:T(8,128)S(1)} %get-tuple-element.28, s32[1024]{0:T(1024)S(1)} %get-tuple-element.44), kind=kCustom, calls=%fused_computation.7 | custom fusion | bytes 461952 | tf_op jit(solution)/shard_map/gather | solution.py:41
  49.1 3.5 %gather_fusion.5 = f32[288,200]{1,0:T(8,128)} fusion(f32[1440,200]{1,0:T(8,128)} %get-tuple-element.26, s32[1024]{0:T(1024)S(1)} %get-tuple-element.45), kind=kCustom, calls=%fused_computation.5 | custom fusion | bytes 461952 | tf_op jit(solution)/shard_map/gather | solution.py:42
  52.6 2.1 %gather_fusion.6 = f32[288,200]{1,0:T(8,128)} fusion(f32[1440,200]{1,0:T(8,128)S(1)} %get-tuple-element.27, s32[1024]{0:T(1024)S(1)} %get-tuple-element.45), kind=kCustom, calls=%fused_computation.6 | custom fusion | bytes 461952 | tf_op jit(solution)/shard_map/gather | solution.py:43
  54.7 3.0 %gather_fusion.2 = f32[288,200]{1,0:T(8,128)S(1)} fusion(f32[1440,200]{1,0:T(8,128)} %get-tuple-element.26, s32[1024]{0:T(1024)S(1)} %copy-done.11), kind=kCustom, calls=%fused_computation.2 | custom fusion | bytes 461952 | tf_op jit(solution)/shard_map/gather | solution.py:42
  57.7 2.1 %gather_fusion.3 = f32[288,200]{1,0:T(8,128)} fusion(f32[1440,200]{1,0:T(8,128)S(1)} %get-tuple-element.27, s32[1024]{0:T(1024)S(1)} %copy-done.11), kind=kCustom, calls=%fused_computation.3 | custom fusion | bytes 461952 | tf_op jit(solution)/shard_map/gather | solution.py:43
  59.9 2.1 %gather_fusion.1 = f32[288,200]{1,0:T(8,128)} fusion(f32[1440,200]{1,0:T(8,128)S(1)} %get-tuple-element.28, s32[1024]{0:T(1024)S(1)} %copy-done.11), kind=kCustom, calls=%fused_computation.1 | custom fusion | bytes 461952 | tf_op jit(solution)/shard_map/gather | solution.py:41
  62.1 2.1 %gather_fusion.4 = f32[288,200]{1,0:T(8,128)} fusion(f32[1440,200]{1,0:T(8,128)S(1)} %get-tuple-element.28, s32[1024]{0:T(1024)S(1)} %copy-done.10), kind=kCustom, calls=%fused_computation.4 | custom fusion | bytes 461952 | tf_op jit(solution)/shard_map/gather | solution.py:41
  67.4 10.3 %scatter_custom_fusion = f32[1440,200]{1,0:T(8,128)S(1)} fusion(s32[1152]{0:T(1024)} %reduce.16, f32[288,200]{1,0:T(8,128)S(1)} %add_multiply_fusion, f32[]{:T(128)} %constant.59, f32[288,200]{1,0:T(8,128)S(1)} %add_multiply_fusion.1, f32[288,200]{1,0:T(8,128)S(1)} %add_multiply_fusion.2, f32[288,200]{1,0:T(8,128)S(1)} %add_multiply_fusion.3, ...), kind=kCustom, calls=%fused_computation.35 | custom fusion | flops 921600 | bytes 2074624 | tf_op jit(solution)/shard_map/add | solution.py:46
  79.2 2.9 %collective-permute-start.6 = (f32[288,200]{1,0:T(8,128)}, f32[288,200]{1,0:T(8,128)S(1)}, u32[]{:S(2)}, u32[]{:S(2)}) collective-permute-start(f32[288,200]{1,0:T(8,128)} %get-tuple-element.23), channel_id=1, source_target_pairs={{0,1},{1,2},{2,3},{3,4},{4,5},{5,6},{6,7},{7,8},{8,9},{9,10},{10,1... | collective-permute-start | bytes 691208 | tf_op jit(solution)/shard_map/ppermute | solution.py:11
  82.1 4.6 %collective-permute-start.5 = (f32[288,200]{1,0:T(8,128)S(1)}, f32[288,200]{1,0:T(8,128)S(1)}, u32[]{:S(2)}, u32[]{:S(2)}) collective-permute-start(f32[288,200]{1,0:T(8,128)S(1)} %get-tuple-element.24), channel_id=1, source_target_pairs={{0,14},{1,15},{2,0},{3,1},{4,2},{5,3},{6,4},{7,5},{8,6},{9,7},{10,... | collective-permute-start | bytes 691208 | tf_op jit(solution)/shard_map/ppermute | solution.py:11
  87.0 8.4 %collective-permute-done.4 = f32[288,200]{1,0:T(8,128)S(1)} collective-permute-done((f32[288,200]{1,0:T(8,128)}, f32[288,200]{1,0:T(8,128)S(1)}, u32[]{:S(2)}, u32[]{:S(2)}) %collective-permute-start.4) | collective-permute-done | bytes 230432 | tf_op jit(solution)/shard_map/ppermute | solution.py:11
  95.4 3.6 %collective-permute-done.6 = f32[288,200]{1,0:T(8,128)S(1)} collective-permute-done((f32[288,200]{1,0:T(8,128)}, f32[288,200]{1,0:T(8,128)S(1)}, u32[]{:S(2)}, u32[]{:S(2)}) %collective-permute-start.6) | collective-permute-done | bytes 230432 | tf_op jit(solution)/shard_map/ppermute | solution.py:11
  100.4 9.0 %scatter_fusion = f32[288,200]{1,0:T(8,128)S(1)} fusion(f32[288,200]{1,0:T(8,128)S(1)} %get-tuple-element.25, s32[1152]{0:T(1024)S(1)} %fusion.21, f32[1152,200]{1,0:T(8,128)S(1)} %bitcast_multiply_fusion), kind=kCustom, calls=%fused_computation.14 | custom fusion | flops 230400 | bytes 2769408 | tf_op jit(solution)/shard_map/scatter-add | solution.py:68
  (110 shorter events, 15.7 us)
Async XLA Ops:
  5.6 5.5 %copy-start.14 = (f32[2,288,4]{1,2,0:T(4,128)S(1)}, f32[2,288,4]{1,2,0:T(4,128)}, u32[]{:S(2)}) copy-start(f32[2,288,4]{1,2,0:T(4,128)} %param.11) | copy-start | bytes 27652
  5.6 5.5 %copy-start.28 = (s32[288,4]{0,1:T(4,128)S(1)}, s32[288,4]{0,1:T(4,128)}, u32[]{:S(2)}) copy-start(s32[288,4]{0,1:T(4,128)} %param.9) | copy-start | bytes 13828
  5.6 7.1 %copy-start.27 = (f32[288,4]{0,1:T(4,128)S(1)}, f32[288,4]{0,1:T(4,128)}, u32[]{:S(2)}) copy-start(f32[288,4]{0,1:T(4,128)} %param.10) | copy-start | bytes 13828
  5.7 16.5 %collective-permute-start = (f32[288,200]{1,0:T(8,128)S(1)}, f32[288,200]{1,0:T(8,128)S(1)}, u32[]{:S(2)}, u32[]{:S(2)}) collective-permute-start(f32[288,200]{1,0:T(8,128)S(1)} %get-tuple-element.33), channel_id=1, source_target_pairs={{0,1},{1,2},{2,3},{3,4},{4,5},{5,6},{6,7},{7,8},{8,9},{9,10},{10,1... | collective-permute-start | bytes 691208 | tf_op jit(solution)/shard_map/ppermute | solution.py:11
  7.5 18.2 %collective-permute-start.3 = (f32[288,200]{1,0:T(8,128)S(1)}, f32[288,200]{1,0:T(8,128)S(1)}, u32[]{:S(2)}, u32[]{:S(2)}) collective-permute-start(f32[288,200]{1,0:T(8,128)S(1)} %get-tuple-element.34), channel_id=1, source_target_pairs={{0,14},{1,15},{2,0},{3,1},{4,2},{5,3},{6,4},{7,5},{8,6},{9,7},{10,... | collective-permute-start | bytes 691208 | tf_op jit(solution)/shard_map/ppermute | solution.py:11
  10.5 17.9 %collective-permute-start.2 = (f32[288,200]{1,0:T(8,128)S(1)}, f32[288,200]{1,0:T(8,128)S(1)}, u32[]{:S(2)}, u32[]{:S(2)}) collective-permute-start(f32[288,200]{1,0:T(8,128)S(1)} %get-tuple-element.35), channel_id=1, source_target_pairs={{0,15},{1,0},{2,1},{3,2},{4,3},{5,4},{6,5},{7,6},{8,7},{9,8},{10,9... | collective-permute-start | bytes 691208 | tf_op jit(solution)/shard_map/ppermute | solution.py:11
  11.0 17.3 %collective-permute-start.1 = (f32[288,200]{1,0:T(8,128)S(1)}, f32[288,200]{1,0:T(8,128)S(1)}, u32[]{:S(2)}, u32[]{:S(2)}) collective-permute-start(f32[288,200]{1,0:T(8,128)S(1)} %get-tuple-element.36), channel_id=1, source_target_pairs={{0,2},{1,3},{2,4},{3,5},{4,6},{5,7},{6,8},{7,9},{8,10},{9,11},{10,... | collective-permute-start | bytes 691208 | tf_op jit(solution)/shard_map/ppermute | solution.py:11
  11.7 40.9 %copy-start.9 = (s32[1024]{0:T(1024)}, s32[1024]{0:T(1024)S(1)}, u32[]{:S(2)}) copy-start(s32[1024]{0:T(1024)S(1)} %get-tuple-element.45) | copy-start | bytes 12292
  62.0 3.6 %copy-start.3 = (f32[288,200]{1,0:T(8,128)S(1)}, f32[288,200]{1,0:T(8,128)}, u32[]{:S(2)}) copy-start(f32[288,200]{1,0:T(8,128)} %gather_fusion.8) | copy-start | bytes 691204
  62.0 3.6 %copy-start.4 = (f32[288,200]{1,0:T(8,128)S(1)}, f32[288,200]{1,0:T(8,128)}, u32[]{:S(2)}) copy-start(f32[288,200]{1,0:T(8,128)} %gather_fusion.9) | copy-start | bytes 691204
  62.1 3.6 %copy-start.19 = (f32[288]{0:T(512)S(1)}, f32[288]{0:T(512)}, u32[]{:S(2)}) copy-start(f32[288]{0:T(512)} %get-tuple-element.15) | copy-start | bytes 3460
  62.1 3.6 %copy-start.20 = (f32[288]{0:T(512)S(1)}, f32[288]{0:T(512)}, u32[]{:S(2)}) copy-start(f32[288]{0:T(512)} %get-tuple-element.52) | copy-start | bytes 3460
  62.1 3.6 %copy-start.25 = (f32[288]{0:T(512)S(1)}, f32[288]{0:T(512)}, u32[]{:S(2)}) copy-start(f32[288]{0:T(512)} %get-tuple-element.8) | copy-start | bytes 3460
  64.2 2.7 %copy-start.5 = (f32[288,200]{1,0:T(8,128)S(1)}, f32[288,200]{1,0:T(8,128)}, u32[]{:S(2)}) copy-start(f32[288,200]{1,0:T(8,128)} %gather_fusion.5) | copy-start | bytes 691204
  64.2 2.7 %copy-start.6 = (f32[288,200]{1,0:T(8,128)S(1)}, f32[288,200]{1,0:T(8,128)}, u32[]{:S(2)}) copy-start(f32[288,200]{1,0:T(8,128)} %gather_fusion.6) | copy-start | bytes 691204
  64.2 2.7 %copy-start.8 = (f32[288,200]{1,0:T(8,128)S(1)}, f32[288,200]{1,0:T(8,128)}, u32[]{:S(2)}) copy-start(f32[288,200]{1,0:T(8,128)} %gather_fusion.4) | copy-start | bytes 691204
  64.2 2.7 %copy-start.17 = (f32[288]{0:T(512)S(1)}, f32[288]{0:T(512)}, u32[]{:S(2)}) copy-start(f32[288]{0:T(512)} %get-tuple-element.16) | copy-start | bytes 3460
  64.2 2.7 %copy-start.18 = (f32[288]{0:T(512)S(1)}, f32[288]{0:T(512)}, u32[]{:S(2)}) copy-start(f32[288]{0:T(512)} %get-tuple-element.51) | copy-start | bytes 3460
  64.2 2.7 %copy-start.24 = (f32[288]{0:T(512)S(1)}, f32[288]{0:T(512)}, u32[]{:S(2)}) copy-start(f32[288]{0:T(512)} %get-tuple-element.6) | copy-start | bytes 3460
  77.7 9.0 %copy-start.13 = (s32[4,32]{1,0:T(4,128)S(1)}, s32[4,32]{1,0:T(4,128)}, u32[]{:S(2)}) copy-start(s32[4,32]{1,0:T(4,128)} %copy-done.12) | copy-start | bytes 1540
  78.6 16.8 %collective-permute-start.4 = (f32[288,200]{1,0:T(8,128)}, f32[288,200]{1,0:T(8,128)S(1)}, u32[]{:S(2)}, u32[]{:S(2)}) collective-permute-start(f32[288,200]{1,0:T(8,128)} %get-tuple-element.21), channel_id=1, source_target_pairs={{0,15},{1,0},{2,1},{3,2},{4,3},{5,4},{6,5},{7,6},{8,7},{9,8},{10,9... | collective-permute-start | bytes 691208 | tf_op jit(solution)/shard_map/ppermute | solution.py:11
  78.6 16.8 %collective-permute-start.7 = (f32[288,200]{1,0:T(8,128)}, f32[288,200]{1,0:T(8,128)S(1)}, u32[]{:S(2)}, u32[]{:S(2)}) collective-permute-start(f32[288,200]{1,0:T(8,128)} %get-tuple-element.22), channel_id=1, source_target_pairs={{0,2},{1,3},{2,4},{3,5},{4,6},{5,7},{6,8},{7,9},{8,10},{9,11},{10,... | collective-permute-start | bytes 691208 | tf_op jit(solution)/shard_map/ppermute | solution.py:11
  79.2 19.8 %collective-permute-start.6 = (f32[288,200]{1,0:T(8,128)}, f32[288,200]{1,0:T(8,128)S(1)}, u32[]{:S(2)}, u32[]{:S(2)}) collective-permute-start(f32[288,200]{1,0:T(8,128)} %get-tuple-element.23), channel_id=1, source_target_pairs={{0,1},{1,2},{2,3},{3,4},{4,5},{5,6},{6,7},{7,8},{8,9},{9,10},{10,1... | collective-permute-start | bytes 691208 | tf_op jit(solution)/shard_map/ppermute | solution.py:11
  82.1 18.0 %collective-permute-start.5 = (f32[288,200]{1,0:T(8,128)S(1)}, f32[288,200]{1,0:T(8,128)S(1)}, u32[]{:S(2)}, u32[]{:S(2)}) collective-permute-start(f32[288,200]{1,0:T(8,128)S(1)} %get-tuple-element.24), channel_id=1, source_target_pairs={{0,14},{1,15},{2,0},{3,1},{4,2},{5,3},{6,4},{7,5},{8,6},{9,7},{10,... | collective-permute-start | bytes 691208 | tf_op jit(solution)/shard_map/ppermute | solution.py:11
  (15 other events, 25.8 us)
where the time goes:
time: 112 us; the launch traced here: 110 us
  local copies, waits for them, and re-layouts  37.8 us (34%)
  other arithmetic  30.9 us (28%)
  waiting for transfers between devices  27.5 us (25%)
  starting transfers between devices  13.4 us (12%)
    ppermute x8, waiting for transfers between devices, from_behind(): return lax.ppermute(x, axis, [(i, (i + by) % count) for i in range(count)])  27.5 us
    gather x4, local copies, waits for them, and re-layouts, transport(): slope_x[source]  13.5 us
    ppermute x8, starting transfers between devices, from_behind(): return lax.ppermute(x, axis, [(i, (i + by) % count) for i in range(count)])  13.4 us
    add x1, other arithmetic, transport(): outflow + jax.ops.segment_sum(flux, source, num_segments=total_cells)  10.3 us
    scatter-add x1, other arithmetic, local(): owned = owned.at[cell_ids.reshape(-1)].add(back.reshape(-1, width))  9.01 us
    gather x4, local copies, waits for them, and re-layouts, transport(): slope_y[source]  8.54 us
    gather x4, local copies, waits for them, and re-layouts, transport(): extended[source] + moment_x[:, column, None] * slope_x[source]  8.53 us
    select_n x1, other arithmetic, build_slopes(): jnp.where(column == 0, right - values, jnp.where(column == 1, 0.5 * (righ...  4.12 us
  transfers between devices with their start and end apart: 8, of which 6 were waited for; matrix products, arithmetic and copies ran while one was open for 3% of the time, Pallas kernels for 0%

commit v1 on v0

v1 whole, which is shorter than its diff:
```python
import functools

import jax
import jax.numpy as jnp
from jax import lax
from jax.experimental import pallas as pl
from jax.experimental.pallas import tpu as pltpu
from jax.sharding import PartitionSpec as P

LANES = 128
F32 = jnp.float32
BF16 = jnp.bfloat16


def round8(n):
    return -(-n // 8) * 8


class Plan:
    def __init__(self, cells, width, elements, slots):
        self.cells, self.width, self.elements, self.slots = cells, width, elements, slots
        self.full = width // LANES
        rest = width % LANES
        self.rest = rest
        self.parts = []
        row = self.full * cells
        lane, size = 0, LANES // 2
        while rest:
            if rest >= size:
                groups = LANES // size
                height = round8(-(-cells // groups))
                self.parts.append((lane, size, height, row))
                row += height
                lane += size
                rest -= size
            size //= 2
        self.table = row
        self.rows = row + slots
        self.group = LANES // 4
        self.tiles = self.full + (1 if self.parts else 0)

    def pack(self, tile_rows, out):
        cells = self.cells
        for t in range(self.full):
            out[t * cells:(t + 1) * cells, :] = tile_rows(t)
        if not self.parts:
            return
        last = tile_rows(self.full)
        for lane, size, height, first in self.parts:
            lanes = lax.broadcasted_iota(jnp.int32, (height, LANES), 1)
            total = None
            for g in range(-(-cells // height)):
                count = min(height, cells - g * height)
                piece = last[g * height:g * height + count]
                shift = (g * size - lane) % LANES
                if shift:
                    piece = pltpu.roll(piece, shift, 1)
                if count < height:
                    piece = jnp.concatenate([piece, jnp.zeros((height - count, LANES), F32)], axis=0)
                total = piece if total is None else jnp.where(lanes >= g * size, piece, total)
            out[first:first + height, :] = total

    def unpack(self, ref):
        cells = self.cells
        tiles = [ref[t * cells:(t + 1) * cells, :] for t in range(self.full)]
        if self.parts:
            last = None
            for lane, size, height, first in self.parts:
                block = ref[first:first + height, :]
                pieces = []
                for g in range(-(-cells // height)):
                    shift = (lane - g * size) % LANES
                    piece = pltpu.roll(block, shift, 1) if shift else block
                    pieces.append(piece[:min(height, cells - g * height)])
                piece = jnp.concatenate(pieces, axis=0)
                lanes = lax.broadcasted_iota(jnp.int32, (cells, LANES), 1)
                last = piece if last is None else jnp.where(lanes >= lane, piece, last)
            tiles.append(last)
        return tiles


def split(x):
    high = x.astype(BF16)
    return high, (x - high.astype(F32)).astype(BF16)


def dot(a, b):
    return jnp.dot(a, b, preferred_element_type=F32)


def element_and_place(src):
    elem = ((src.astype(F32) + 0.5) * (1.0 / 9.0)).astype(jnp.int32)
    return elem, src - 9 * elem


def pack_kernel(plan, q_ref, src_ref, fr_ref, mo_ref, ids_ref, cnt_ref, out_ref, own_ref, t_ref):
    cells, E, S = plan.cells, plan.elements, plan.slots
    for t in range(plan.full):
        t_ref[t] = q_ref[:, t * LANES:(t + 1) * LANES]
    if plan.rest:
        t_ref[plan.full, :, 0:plan.rest] = q_ref[:, plan.full * LANES:plan.width]

    def tile_rows(t):
        return jnp.concatenate([t_ref[t, pl.ds(p, E, stride=9), :] for p in range(9)], axis=0)

    plan.pack(tile_rows, out_ref)
    elem, place = element_and_place(src_ref[...])
    fr = fr_ref[...]
    wx = fr * mo_ref[0]
    wy = fr * mo_ref[1]
    total = E + 4 * S
    erow = lax.broadcasted_iota(jnp.int32, (total, cells), 0)
    urow = lax.broadcasted_iota(jnp.int32, (32, cells), 0)
    uplace = urow - jnp.where(urow < 9, 0, jnp.where(urow < 18, 9, 18))
    acc = None
    for k in range(src_ref.shape[0]):
        hot = jnp.where(erow == elem[k:k + 1, :], 1.0, 0.0).astype(BF16)
        value = jnp.where(urow < 9, fr[k:k + 1, :], jnp.where(urow < 18, wx[k:k + 1, :], wy[k:k + 1, :]))
        value = jnp.where(uplace == place[k:k + 1, :], value, 0.0)
        high, low = split(value)
        both = jnp.concatenate([high, low, jnp.zeros((64, cells), BF16)], axis=0)
        got = lax.dot_general(hot, both, (((1,), (1,)), ((), ())), preferred_element_type=F32)
        acc = got if acc is None else acc + got
    acc = acc + pltpu.roll(acc, LANES - 32, 1)
    own_ref[...] = acc[0:E]
    lane = lax.broadcasted_iota(jnp.int32, (S, LANES), 1)
    table = jnp.zeros((S, LANES), F32)
    diag = lax.broadcasted_iota(jnp.int32, (S, S), 0) == lax.broadcasted_iota(jnp.int32, (S, S), 1)
    slot = lax.broadcasted_iota(jnp.int32, (1, S), 1)
    for o in range(4):
        part = acc[E + o * S:E + (o + 1) * S]
        if o:
            part = pltpu.roll(part, plan.group * o, 1)
        inside = (lane >= plan.group * o) & (lane < plan.group * o + 27)
        table = jnp.where(inside, part, table)
        ids = jnp.where(slot < cnt_ref[o], ids_ref[o:o + 1, :].astype(F32), -1.0)
        column = jnp.sum(jnp.where(diag, ids, 0.0), axis=1, keepdims=True)
        table = jnp.where(lane == plan.group * o + 27, column, table)
    out_ref[plan.table:plan.table + S, :] = table


def matrix_kernel(plan, src_ref, fr_ref, mo_ref, hi_ref, lo_ref, col_ref):
    cells, E = plan.cells, plan.elements
    K = src_ref.shape[0]
    elem, place = element_and_place(src_ref[...])
    fr = fr_ref[...]
    wx = fr * mo_ref[0]
    wy = fr * mo_ref[1]
    row = jnp.where(place >= 6, 2, jnp.where(place >= 3, 1, 0))
    r = row.astype(F32)
    c = (place - 3 * row).astype(F32)
    centre = fr + wx * (c - 1.0) + wy * (r - 1.0)
    rows = [
        elem.astype(F32), place.astype(F32), centre,
        wx * (1.0 - 0.5 * c), wx * (-0.5 * c), wy * (1.0 - 0.5 * r), wy * (-0.5 * r),
    ]
    rows = jnp.concatenate(rows + [jnp.zeros((LANES - 7 * K, cells), F32)], axis=0)
    pad = -cells % LANES
    if pad:
        rows = jnp.concatenate([rows, jnp.zeros((LANES, pad), F32)], axis=1)
    col_ref[...] = jnp.transpose(rows, (1, 0))[0:cells]
    step = E
    lane = lax.broadcasted_iota(jnp.int32, (step, LANES), 1)
    per = LANES // E
    lists = hi_ref.shape[0]

    def body(i, carry):
        at = pl.multiple_of(i * step, step)
        cols = col_ref[pl.ds(at, step), :]

        def wide(n, k):
            return jnp.broadcast_to(cols[:, n * K + k:n * K + k + 1], (step, LANES))

        for t in range(-(-9 // per)):
            where = (lane // E + per * t).astype(F32)
            inner = (lane % E).astype(F32)
            sums = [jnp.zeros((step, LANES), F32) for _ in range(lists)]
            for k in range(K):
                d = where - wide(1, k)
                coef = jnp.where(d == 0.0, wide(2, k), 0.0)
                coef = jnp.where(d == 1.0, wide(3, k), coef)
                coef = jnp.where(d == -1.0, wide(4, k), coef)
                coef = jnp.where(d == 3.0, wide(5, k), coef)
                coef = jnp.where(d == -3.0, wide(6, k), coef)
                e = wide(0, k) - inner
                for n in range(lists):
                    sums[n] = sums[n] + jnp.where(e == float(n * E), coef, 0.0)
            size = min(LANES, 9 * E - t * LANES)
            for n in range(lists):
                high, low = split(sums[n])
                hi_ref[n, pl.ds(at, step), t * LANES:t * LANES + size] = high[:, :size]
                lo_ref[n, pl.ds(at, step), t * LANES:t * LANES + size] = low[:, :size]
        return carry

    lax.fori_loop(0, cells // step, body, 0)


def apply_block(plan, tiles, ids, hi, lo):
    E, S = plan.elements, plan.slots
    masses = jnp.concatenate(tiles, axis=1)
    high, low = split(masses)
    if ids is not None:
        per = LANES // E
        r = lax.broadcasted_iota(jnp.int32, (LANES, LANES), 0)
        l = lax.broadcasted_iota(jnp.int32, (LANES, LANES), 1)
        many = jnp.concatenate([ids] * per, axis=0)
        hot = jnp.where(((l % E).astype(F32) == many) & (r // E == l // E), 1.0, 0.0).astype(BF16)
        pair = jnp.concatenate([high, low], axis=1)
        pieces = []
        for first in range(0, plan.cells, LANES):
            size = min(LANES, plan.cells - first)
            pieces.append(dot(hot[:size, :size], pair[first:first + size]).astype(BF16))
        pair = jnp.concatenate(pieces, axis=0)
        high, low = pair[:, :masses.shape[1]], pair[:, masses.shape[1]:]
    return dot(hi, high) + dot(hi, low) + dot(lo, high)


def table_ids(plan, table, which):
    lane = lax.broadcasted_iota(jnp.int32, table.shape, 1)
    return jnp.sum(jnp.where(lane == plan.group * which + 27, table, 0.0), axis=1, keepdims=True)


def returned_weights(plan, table, which, ids_ref, cnt_ref):
    E, S = plan.elements, plan.slots
    part = pltpu.roll(table, lax.rem(LANES - plan.group * which, LANES), 1)
    lane = lax.broadcasted_iota(jnp.int32, (S, LANES), 1)
    part = jnp.where(lane < 27, part, 0.0)
    high, low = split(part)
    slot = lax.broadcasted_iota(jnp.int32, (E, S), 1)
    e = lax.broadcasted_iota(jnp.int32, (E, S), 0)
    live = (e == ids_ref[pl.ds(which, 1), :]) & (slot < cnt_ref[which])
    hot = jnp.where(live, 1.0, 0.0).astype(BF16)
    return dot(hot, high) + dot(hot, low)


def kept(plan, tiles, weights, out_ref):
    E = plan.elements
    for p in range(9):
        w = [jnp.broadcast_to(weights[:, 9 * j + p:9 * j + p + 1], (E, LANES)) for j in range(3)]
        for t in range(plan.tiles):
            def at(i):
                return tiles[t][i * E:(i + 1) * E]

            def slope(pos, step):
                if pos == 0:
                    return at(p + step) - at(p)
                if pos == 1:
                    return 0.5 * (at(p + step) - at(p - step))
                return at(p) - at(p - step)

            value = at(p) - (w[0] * at(p) + w[1] * slope(p % 3, 1) + w[2] * slope(p // 3, 3))
            out_ref[t, pl.ds(p, E, stride=9), :] = value


def final_kernel(plan, ids_ref, cnt_ref, own_w_ref, own_ref, x_ref, s_ref, y_ref, f_ref,
                 hi_ref, lo_ref, out_ref, t_ref):
    S = plan.slots
    odd = lax.rem(lax.axis_index("curve"), 2)
    tiles = plan.unpack(own_ref)
    inflow = apply_block(plan, tiles, None, hi_ref[0], lo_ref[0])
    weights = own_w_ref[...]
    for ref, even_list, odd_list in ((s_ref, 0, 2), (x_ref, 1, 3), (f_ref, 2, 0), (y_ref, 3, 1)):
        mine = jnp.where(odd == 1, odd_list, even_list)
        theirs = lax.rem(mine + 2, 4)
        table = ref[plan.table:plan.table + S, :]
        weights = weights + returned_weights(plan, table, mine, ids_ref, cnt_ref)
        ids = table_ids(plan, table, theirs)
        inflow = inflow + apply_block(plan, plan.unpack(ref), ids, hi_ref[theirs + 1], lo_ref[theirs + 1])
    kept(plan, tiles, weights, t_ref)
    for t in range(plan.full):
        out_ref[:, t * LANES:(t + 1) * LANES] = t_ref[t] + inflow[:, t * LANES:(t + 1) * LANES]
    if plan.rest:
        at = plan.full * LANES
        out_ref[:, at:plan.width] = (t_ref[plan.full] + inflow[:, at:at + LANES])[:, :plan.rest]


def send(x, table):
    return lax.ppermute(x, "curve", table)


def local(tracer_mass, send_ids, send_counts, sources, fractions, moments):
    count = lax.axis_size("curve")
    cells, width = tracer_mass.shape
    slots = send_ids.shape[1]
    elements = cells // 9
    plan = Plan(cells, width, elements, slots)
    src, fr, mo = sources.T, fractions.T, jnp.transpose(moments, (0, 2, 1))
    vmem = pl.BlockSpec(memory_space=pltpu.VMEM)
    smem = pl.BlockSpec(memory_space=pltpu.SMEM)
    payload, own_w = pl.pallas_call(
        functools.partial(pack_kernel, plan),
        out_shape=(
            jax.ShapeDtypeStruct((plan.rows, LANES), F32),
            jax.ShapeDtypeStruct((elements, LANES), F32),
        ),
        in_specs=[vmem] * 5 + [smem],
        out_specs=(vmem, vmem),
        scratch_shapes=[pltpu.VMEM((plan.tiles, cells, LANES), F32)],
        name="pack",
    )(tracer_mass, src, fr, mo, send_ids, send_counts)
    towards = [(i, (i + (2 if i % 2 else -2)) % count) for i in range(count)]
    away = [(i, (i - (2 if i % 2 else -2)) % count) for i in range(count)]
    swap = [(i, i ^ 1) for i in range(count)]
    got_x = send(payload, towards)
    got_s = send(payload, swap)
    got_y = send(payload, away)
    got_f = send(got_x, swap)
    hi, lo = pl.pallas_call(
        functools.partial(matrix_kernel, plan),
        out_shape=(jax.ShapeDtypeStruct((5, cells, cells), BF16),) * 2,
        in_specs=[vmem] * 3,
        out_specs=(vmem, vmem),
        scratch_shapes=[pltpu.VMEM((cells, LANES), F32)],
        cost_estimate=pl.CostEstimate(flops=2 * 10**9, bytes_accessed=2 * 10**6, transcendentals=0),
        name="matrix",
    )(src, fr, mo)
    return pl.pallas_call(
        functools.partial(final_kernel, plan),
        out_shape=jax.ShapeDtypeStruct((cells, width), F32),
        in_specs=[vmem, smem] + [vmem] * 8,
        out_specs=vmem,
        scratch_shapes=[pltpu.VMEM((plan.tiles, cells, LANES), F32)],
        name="final",
    )(send_ids, send_counts, own_w, payload, got_x, got_s, got_y, got_f, hi, lo)


def solution(mesh):
    placed = (
        P(("groups", "curve"), None),
        P(("groups", "curve"), None),
        P(("groups", "curve")),
        P(("groups", "curve"), None),
        P(("groups", "curve"), None),
        P(None, ("groups", "curve"), None),
    )
    return jax.shard_map(
        local, mesh=mesh, in_specs=placed, out_specs=P(("groups", "curve"), None), check_vma=False
    )
```

time: 112 us -> 29 us (0.26); the launches traced: 110 us -> 28.7 us
  local copies, waits for them, and re-layouts: 37.8 us -> 0.86 us
  other arithmetic: 30.9 us -> 0 us
  waiting for transfers between devices: 27.5 us -> 5.41 us
  Pallas kernels: 0 us -> 12.7 us
  starting transfers between devices: 13.4 us -> 9.68 us
    gather x13 -> x0, local copies, waits for them, and re-layouts: 33.8 us -> none  [the longest x4 13.5 us: transport(): slope_x[source]]
    ppermute x8 -> x4, waiting for transfers between devices: 27.5 us -> 5.41 us  [send(): return lax.ppermute(x, 'curve', table)]
    pallas_call x0 -> x3, Pallas kernels: none -> 12.7 us  [the longest x1 5.76 us: local(): pl.pallas_call(functools.partial(final_kernel, plan), out_shape=jax.Shape...]
    add x2 -> x0, other arithmetic: 10.3 us -> none  [the longest x1 10.3 us: transport(): outflow + jax.ops.segment_sum(flux, source, num_segments=total_cells)]
    scatter-add x1 -> x0, other arithmetic: 9.01 us -> none  [local(): owned = owned.at[cell_ids.reshape(-1)].add(back.reshape(-1, width))]
    select_n x4 -> x0, other arithmetic: 4.19 us -> none  [the longest x1 4.12 us: build_slopes(): jnp.where(column == 0, right - values, jnp.where(column == 1, 0.5 * (righ...]
    mul x7 -> x0, other arithmetic: 4.02 us -> none  [the longest x4 2.86 us: transport(): fraction_dev[:, column, None]]
    ppermute x8 -> x4, starting transfers between devices: 13.4 us -> 9.68 us  [send(): return lax.ppermute(x, 'curve', table)]
  transfers between devices with their start and end apart: 8 -> 4, of which waited for: 6 -> 1; matrix products, arithmetic and copies ran while one was open for 3% -> 0% of each run, Pallas kernels for 0% -> 17%
where the time goes in v1:
time: 29 us; the launch traced here: 28.7 us
  Pallas kernels  12.7 us (44%)
  starting transfers between devices  9.68 us (33%)
  waiting for transfers between devices  5.41 us (19%)
  local copies, waits for them, and re-layouts  0.86 us (3%)
    ppermute x4, starting transfers between devices, send(): return lax.ppermute(x, 'curve', table)  9.68 us
    pallas_call x1, Pallas kernels, local(): pl.pallas_call(functools.partial(final_kernel, plan), out_shape=jax.Shape...  5.76 us
    ppermute x4, waiting for transfers between devices, send(): return lax.ppermute(x, 'curve', table)  5.41 us
    pallas_call x1, Pallas kernels, local(): pl.pallas_call(functools.partial(matrix_kernel, plan), out_shape=(jax.Sha...  4.79 us
    pallas_call x1, Pallas kernels, local(): pl.pallas_call(functools.partial(pack_kernel, plan), out_shape=(jax.Shape...  2.18 us
    unnamed x8, local copies, waits for them, and re-layouts  0.86 us
  transfers between devices with their start and end apart: 4, of which 1 were waited for; matrix products, arithmetic and copies ran while one was open for 0% of the time, Pallas kernels for 17%

profile of v1, /device:TPU:5, one launch (start us, length us, event | category | flops | bytes accessed | tf_op | source)
XLA Modules:
  0.0 28.7 jit_solution(13087778869904548960)
XLA Ops:
  0.0 2.2 %pack.1 = (f32[488,128]{1,0:T(8,128)}, f32[32,128]{1,0:T(8,128)}) custom-call(f32[288,200]{1,0:T(8,128)} %q_ref.1, s32[4,288]{1,0:T(4,128)} %bitcast.5, f32[4,288]{1,0:T(4,128)} %bitcast.7, f32[2,4,288]{2,1,0:T(4,128)} %bitcast.3, s32[4,32]{1,0:T(4,128)} %ids_ref.3, s32[4]{0:T(128)} %cnt_ref.3), custom_call_target="tpu_custom_call" | custom-call | tf_op jit(solution)/shard_map/pack/pallas_call | solution.py:290
  2.2 1.2 %collective-permute-start = (f32[488,128]{1,0:T(8,128)}, f32[488,128]{1,0:T(8,128)S(1)}, u32[]{:S(2)}, u32[]{:S(2)}) collective-permute-start(f32[488,128]{1,0:T(8,128)} %get-tuple-element.10.own_ref), channel_id=1, source_target_pairs={{0,14},{1,3},{2,0},{3,5},{4,2},{5,7},{6,4},{7,9},{8,6},{9,11},{10,... | collective-permute-start | bytes 749576 | tf_op jit(solution)/shard_map/ppermute | solution.py:278
  3.4 3.0 %collective-permute-start.2 = (f32[488,128]{1,0:T(8,128)}, f32[488,128]{1,0:T(8,128)S(1)}, u32[]{:S(2)}, u32[]{:S(2)}) collective-permute-start(f32[488,128]{1,0:T(8,128)} %get-tuple-element.10.own_ref), channel_id=1, source_target_pairs={{0,2},{1,15},{2,4},{3,1},{4,6},{5,3},{6,8},{7,5},{8,10},{9,7},{10,... | collective-permute-start | bytes 749576 | tf_op jit(solution)/shard_map/ppermute | solution.py:278
  6.4 1.0 %collective-permute-start.1 = (f32[488,128]{1,0:T(8,128)}, f32[488,128]{1,0:T(8,128)S(1)}, u32[]{:S(2)}, u32[]{:S(2)}) collective-permute-start(f32[488,128]{1,0:T(8,128)} %get-tuple-element.10.own_ref), channel_id=1, source_target_pairs={{0,1},{1,0},{2,3},{3,2},{4,5},{5,4},{6,7},{7,6},{8,9},{9,8},{10,11... | collective-permute-start | bytes 749576 | tf_op jit(solution)/shard_map/ppermute | solution.py:278
  7.4 5.4 %collective-permute-done.x_ref = f32[488,128]{1,0:T(8,128)S(1)} collective-permute-done((f32[488,128]{1,0:T(8,128)}, f32[488,128]{1,0:T(8,128)S(1)}, u32[]{:S(2)}, u32[]{:S(2)}) %collective-permute-start) | collective-permute-done | bytes 249888 | tf_op jit(solution)/shard_map/ppermute | solution.py:278
  12.8 0.0 copy-start
  12.8 4.5 %collective-permute-start.3 = (f32[488,128]{1,0:T(8,128)S(1)}, f32[488,128]{1,0:T(8,128)S(1)}, u32[]{:S(2)}, u32[]{:S(2)}) collective-permute-start(f32[488,128]{1,0:T(8,128)S(1)} %collective-permute-done.x_ref), channel_id=1, source_target_pairs={{0,1},{1,0},{2,3},{3,2},{4,5},{5,4},{6,7},{7,6},{8,9},{9,8},{10,11... | collective-permute-start | bytes 749576 | tf_op jit(solution)/shard_map/ppermute | solution.py:278
  17.3 4.8 %matrix.1 = (bf16[5,288,288]{2,1,0:T(8,128)(2,1)}, bf16[5,288,288]{2,1,0:T(8,128)(2,1)}) custom-call(s32[4,288]{1,0:T(4,128)} %bitcast.6, f32[4,288]{1,0:T(4,128)} %bitcast.8, f32[2,4,288]{2,1,0:T(4,128)} %bitcast.4), custom_call_target="tpu_custom_call" | custom-call | flops 2000000000 | bytes 2000000 | tf_op jit(solution)/shard_map/matrix/pallas_call | solution.py:308
  22.1 0.0 copy-done
  22.1 0.0 collective-permute-done.2.y_ref
  22.1 0.0 copy-start.1
  22.1 0.0 collective-permute-done.1.s_ref
  22.1 0.0 copy-start.2
  22.1 0.0 collective-permute-done.3.f_ref
  22.1 0.0 copy-start.3
  22.1 0.7 %copy-done.1 = f32[488,128]{1,0:T(8,128)} copy-done((f32[488,128]{1,0:T(8,128)}, f32[488,128]{1,0:T(8,128)S(1)}, u32[]{:S(2)}) %copy-start.1) | copy-done | bytes 249880
  22.8 0.1 copy-done.2
  22.9 0.1 copy-done.3
  23.0 5.8 %final.1 = f32[288,200]{1,0:T(8,128)} custom-call(s32[4,32]{1,0:T(4,128)} %ids_ref.3, s32[4]{0:T(128)} %cnt_ref.3, f32[32,128]{1,0:T(8,128)} %get-tuple-element.9.own_w_ref, f32[488,128]{1,0:T(8,128)} %get-tuple-element.10.own_ref, f32[488,128]{1,0:T(8,128)} %copy-done, f32[488,128]{1,0:T(8,128)} %copy-done.2, f32[488,128]{1,0:T(8,128)} %copy-done.1, ...), custom_call_target="tpu_custom_call" | custom-call | tf_op jit(solution)/shard_map/final/pallas_call | solution.py:317
Async XLA Ops:
  2.2 10.6 %collective-permute-start = (f32[488,128]{1,0:T(8,128)}, f32[488,128]{1,0:T(8,128)S(1)}, u32[]{:S(2)}, u32[]{:S(2)}) collective-permute-start(f32[488,128]{1,0:T(8,128)} %get-tuple-element.10.own_ref), channel_id=1, source_target_pairs={{0,14},{1,3},{2,0},{3,5},{4,2},{5,7},{6,4},{7,9},{8,6},{9,11},{10,... | collective-permute-start | bytes 749576 | tf_op jit(solution)/shard_map/ppermute | solution.py:278
  3.4 18.7 %collective-permute-start.2 = (f32[488,128]{1,0:T(8,128)}, f32[488,128]{1,0:T(8,128)S(1)}, u32[]{:S(2)}, u32[]{:S(2)}) collective-permute-start(f32[488,128]{1,0:T(8,128)} %get-tuple-element.10.own_ref), channel_id=1, source_target_pairs={{0,2},{1,15},{2,4},{3,1},{4,6},{5,3},{6,8},{7,5},{8,10},{9,7},{10,... | collective-permute-start | bytes 749576 | tf_op jit(solution)/shard_map/ppermute | solution.py:278
  6.4 15.6 %collective-permute-start.1 = (f32[488,128]{1,0:T(8,128)}, f32[488,128]{1,0:T(8,128)S(1)}, u32[]{:S(2)}, u32[]{:S(2)}) collective-permute-start(f32[488,128]{1,0:T(8,128)} %get-tuple-element.10.own_ref), channel_id=1, source_target_pairs={{0,1},{1,0},{2,3},{3,2},{4,5},{5,4},{6,7},{7,6},{8,9},{9,8},{10,11... | collective-permute-start | bytes 749576 | tf_op jit(solution)/shard_map/ppermute | solution.py:278
  12.8 9.3 %copy-start = (f32[488,128]{1,0:T(8,128)}, f32[488,128]{1,0:T(8,128)S(1)}, u32[]{:S(2)}) copy-start(f32[488,128]{1,0:T(8,128)S(1)} %collective-permute-done.x_ref) | copy-start | bytes 749572
  12.8 9.3 %collective-permute-start.3 = (f32[488,128]{1,0:T(8,128)S(1)}, f32[488,128]{1,0:T(8,128)S(1)}, u32[]{:S(2)}, u32[]{:S(2)}) collective-permute-start(f32[488,128]{1,0:T(8,128)S(1)} %collective-permute-done.x_ref), channel_id=1, source_target_pairs={{0,1},{1,0},{2,3},{3,2},{4,5},{5,4},{6,7},{7,6},{8,9},{9,8},{10,11... | collective-permute-start | bytes 749576 | tf_op jit(solution)/shard_map/ppermute | solution.py:278
  22.1 0.7 %copy-start.1 = (f32[488,128]{1,0:T(8,128)}, f32[488,128]{1,0:T(8,128)S(1)}, u32[]{:S(2)}) copy-start(f32[488,128]{1,0:T(8,128)S(1)} %collective-permute-done.2.y_ref) | copy-start | bytes 749572
  22.1 0.8 %copy-start.2 = (f32[488,128]{1,0:T(8,128)}, f32[488,128]{1,0:T(8,128)S(1)}, u32[]{:S(2)}) copy-start(f32[488,128]{1,0:T(8,128)S(1)} %collective-permute-done.1.s_ref) | copy-start | bytes 749572
  22.1 0.9 %copy-start.3 = (f32[488,128]{1,0:T(8,128)}, f32[488,128]{1,0:T(8,128)S(1)}, u32[]{:S(2)}) copy-start(f32[488,128]{1,0:T(8,128)S(1)} %collective-permute-done.3.f_ref) | copy-start | bytes 749572

commit v2 on v1

--- a/solution.py
+++ b/solution.py
@@ -6,6 +6,7 @@
 from jax.experimental import pallas as pl
 from jax.experimental.pallas import tpu as pltpu
 from jax.sharding import PartitionSpec as P
+
 
 LANES = 128
 F32 = jnp.float32
@@ -93,8 +94,22 @@
     return elem, src - 9 * elem
 
 
-def pack_kernel(plan, q_ref, src_ref, fr_ref, mo_ref, ids_ref, cnt_ref, out_ref, own_ref, t_ref):
-    cells, E, S = plan.cells, plan.elements, plan.slots
+def pack_kernel(plan, q_hbm, src_hbm, fr_hbm, mo_hbm, ids_hbm, cnt_hbm, out_ref, own_ref,
+                src_ref, fr_ref, mo_ref, q_ref, ids_ref, cnt_ref, t_ref, sems):
+    E = plan.elements
+    copies = [
+        pltpu.make_async_copy(a, b, sems.at[n])
+        for n, (a, b) in enumerate((
+            (src_hbm, src_ref), (fr_hbm, fr_ref), (mo_hbm, mo_ref),
+            (cnt_hbm, cnt_ref), (ids_hbm, ids_ref), (q_hbm, q_ref),
+        ))
+    ]
+    for copy in copies:
+        copy.start()
+    for copy in copies[:5]:
+        copy.wait()
+    weights_table(plan, src_ref, fr_ref, mo_ref, ids_ref, cnt_ref, out_ref, own_ref)
+    copies[5].wait()
     for t in range(plan.full):
         t_ref[t] = q_ref[:, t * LANES:(t + 1) * LANES]
     if plan.rest:
@@ -104,6 +119,10 @@
         return jnp.concatenate([t_ref[t, pl.ds(p, E, stride=9), :] for p in range(9)], axis=0)
 
     plan.pack(tile_rows, out_ref)
+
+
+def weights_table(plan, src_ref, fr_ref, mo_ref, ids_ref, cnt_ref, out_ref, own_ref):
+    cells, E, S = plan.cells, plan.elements, plan.slots
     elem, place = element_and_place(src_ref[...])
     fr = fr_ref[...]
     wx = fr * mo_ref[0]
@@ -196,7 +215,7 @@
 
 
 def apply_block(plan, tiles, ids, hi, lo):
-    E, S = plan.elements, plan.slots
+    E = plan.elements
     masses = jnp.concatenate(tiles, axis=1)
     high, low = split(masses)
     if ids is not None:
@@ -220,17 +239,46 @@
     return jnp.sum(jnp.where(lane == plan.group * which + 27, table, 0.0), axis=1, keepdims=True)
 
 
-def returned_weights(plan, table, which, ids_ref, cnt_ref):
-    E, S = plan.elements, plan.slots
+def returned_weights(plan, table, which, hot):
     part = pltpu.roll(table, lax.rem(LANES - plan.group * which, LANES), 1)
-    lane = lax.broadcasted_iota(jnp.int32, (S, LANES), 1)
+    lane = lax.broadcasted_iota(jnp.int32, part.shape, 1)
     part = jnp.where(lane < 27, part, 0.0)
     high, low = split(part)
+    return dot(hot, high) + dot(hot, low)
+
+
+def live_slots(plan, which, ids_ref, cnt_ref):
+    E, S = plan.elements, plan.slots
     slot = lax.broadcasted_iota(jnp.int32, (E, S), 1)
     e = lax.broadcasted_iota(jnp.int32, (E, S), 0)
     live = (e == ids_ref[pl.ds(which, 1), :]) & (slot < cnt_ref[which])
-    hot = jnp.where(live, 1.0, 0.0).astype(BF16)
-    return dot(hot, high) + dot(hot, low)
+    return jnp.where(live, 1.0, 0.0).astype(BF16)
+
+
+def my_list(name, count):
+    index = lax.axis_index("curve")
+    odd = lax.rem(index, 2) == 1
+    end = (index == 0) | (index == count - 1)
+    beside = (index == 1) | (index == count - 2)
+    swap = jnp.where(odd, 2, 0)
+    near = jnp.where(odd, 3, 1)
+    far = jnp.where(odd, 1, 3)
+    if name == "f":
+        return jnp.where(odd, 0, 2)
+    if name == "w":
+        return jnp.where(end, far, jnp.where(beside, near, swap))
+    if name == "x":
+        return jnp.where(beside, swap, near)
+    return jnp.where(end, swap, far)
+
+
+def arrived(plan, mine, block, hot, hi_ref, lo_ref):
+    theirs = lax.rem(mine + 2, 4)
+    table = block[plan.table:plan.rows, :]
+    weights = returned_weights(plan, table, mine, hot)
+    ids = table_ids(plan, table, theirs)
+    inflow = apply_block(plan, plan.unpack(block), ids, hi_ref[theirs + 1], lo_ref[theirs + 1])
+    return inflow, weights
 
 
 def kept(plan, tiles, weights, out_ref):
@@ -252,21 +300,28 @@
             out_ref[t, pl.ds(p, E, stride=9), :] = value
 
 
-def final_kernel(plan, ids_ref, cnt_ref, own_w_ref, own_ref, x_ref, s_ref, y_ref, f_ref,
-                 hi_ref, lo_ref, out_ref, t_ref):
-    S = plan.slots
-    odd = lax.rem(lax.axis_index("curve"), 2)
-    tiles = plan.unpack(own_ref)
-    inflow = apply_block(plan, tiles, None, hi_ref[0], lo_ref[0])
-    weights = own_w_ref[...]
-    for ref, even_list, odd_list in ((s_ref, 0, 2), (x_ref, 1, 3), (f_ref, 2, 0), (y_ref, 3, 1)):
-        mine = jnp.where(odd == 1, odd_list, even_list)
-        theirs = lax.rem(mine + 2, 4)
-        table = ref[plan.table:plan.table + S, :]
-        weights = weights + returned_weights(plan, table, mine, ids_ref, cnt_ref)
-        ids = table_ids(plan, table, theirs)
-        inflow = inflow + apply_block(plan, plan.unpack(ref), ids, hi_ref[theirs + 1], lo_ref[theirs + 1])
-    kept(plan, tiles, weights, t_ref)
+def first_kernel(plan, count, ids_ref, cnt_ref, own_ref, hi_ref, lo_ref, acc_ref, hot_ref):
+    for n, name in enumerate("wxyf"):
+        hot_ref[n] = live_slots(plan, my_list(name, count), ids_ref, cnt_ref)
+    acc_ref[...] = apply_block(plan, plan.unpack(own_ref), None, hi_ref[0], lo_ref[0])
+
+
+def next_kernel(plan, count, names, in_acc_ref, in_w_ref, hot_ref, *refs):
+    blocks, (hi_ref, lo_ref, acc_ref, w_ref) = refs[:len(names)], refs[len(names):]
+    acc, weights = in_acc_ref[...], in_w_ref[...]
+    for name, ref in zip(names, blocks):
+        hot = hot_ref["wxyf".index(name)]
+        more, extra = arrived(plan, my_list(name, count), ref, hot, hi_ref, lo_ref)
+        acc, weights = acc + more, weights + extra
+    acc_ref[...] = acc
+    w_ref[...] = weights
+
+
+def last_kernel(plan, count, name, acc_ref, in_w_ref, hot_ref, own_ref, ref, hi_ref, lo_ref, out_ref, t_ref):
+    hot = hot_ref["wxyf".index(name)]
+    more, weights = arrived(plan, my_list(name, count), ref, hot, hi_ref, lo_ref)
+    inflow = acc_ref[...] + more
+    kept(plan, plan.unpack(own_ref), in_w_ref[...] + weights, t_ref)
     for t in range(plan.full):
         out_ref[:, t * LANES:(t + 1) * LANES] = t_ref[t] + inflow[:, t * LANES:(t + 1) * LANES]
     if plan.rest:
@@ -274,8 +329,20 @@
         out_ref[:, at:plan.width] = (t_ref[plan.full] + inflow[:, at:at + LANES])[:, :plan.rest]
 
 
-def send(x, table):
-    return lax.ppermute(x, "curve", table)
+GRANT = pltpu.CompilerParams(vmem_limit_bytes=8 * 2**20)
+VMEM = pl.BlockSpec(memory_space=pltpu.VMEM)
+SMEM = pl.BlockSpec(memory_space=pltpu.SMEM)
+
+
+HBM = pl.BlockSpec(memory_space=pltpu.HBM)
+
+
+def far(*arrays):
+    return [pltpu.with_memory_space_constraint(a, pltpu.HBM) for a in arrays]
+
+
+def near(*arrays):
+    return [pltpu.with_memory_space_constraint(a, pltpu.VMEM) for a in arrays]
 
 
 def local(tracer_mass, send_ids, send_counts, sources, fractions, moments):
@@ -284,44 +351,88 @@
     slots = send_ids.shape[1]
     elements = cells // 9
     plan = Plan(cells, width, elements, slots)
+    lanes = plan.tiles * LANES
     src, fr, mo = sources.T, fractions.T, jnp.transpose(moments, (0, 2, 1))
-    vmem = pl.BlockSpec(memory_space=pltpu.VMEM)
-    smem = pl.BlockSpec(memory_space=pltpu.SMEM)
-    payload, own_w = pl.pallas_call(
+    masses_t = pltpu.VMEM((cells, lanes), F32)
+    weights_t = pltpu.VMEM((elements, LANES), F32)
+    work_t = pltpu.VMEM((plan.tiles, cells, LANES), F32)
+    payload, own_w, *pieces = pl.pallas_call(
         functools.partial(pack_kernel, plan),
         out_shape=(
-            jax.ShapeDtypeStruct((plan.rows, LANES), F32),
-            jax.ShapeDtypeStruct((elements, LANES), F32),
+            pltpu.VMEM((plan.rows, LANES), F32),
+            weights_t,
+            pltpu.VMEM(src.shape, jnp.int32),
+            pltpu.VMEM(fr.shape, F32),
+            pltpu.VMEM(mo.shape, F32),
         ),
-        in_specs=[vmem] * 5 + [smem],
-        out_specs=(vmem, vmem),
-        scratch_shapes=[pltpu.VMEM((plan.tiles, cells, LANES), F32)],
+        in_specs=[HBM] * 6,
+        out_specs=(VMEM,) * 5,
+        scratch_shapes=[
+            pltpu.VMEM(tracer_mass.shape, F32),
+            pltpu.VMEM(send_ids.shape, jnp.int32),
+            pltpu.SMEM(send_counts.shape, jnp.int32),
+            work_t,
+            pltpu.SemaphoreType.DMA((6,)),
+        ],
+        compiler_params=GRANT,
         name="pack",
-    )(tracer_mass, src, fr, mo, send_ids, send_counts)
-    towards = [(i, (i + (2 if i % 2 else -2)) % count) for i in range(count)]
-    away = [(i, (i - (2 if i % 2 else -2)) % count) for i in range(count)]
+    )(*far(tracer_mass, src, fr, mo, send_ids, send_counts))
+
+    def steps(by):
+        pairs = [(i, i + (by if i % 2 else -by)) for i in range(count)]
+        inside = [(i, j if 0 <= j < count else i ^ 1) for i, j in pairs]
+        return inside, [(i, j % count) for i, j in pairs if not 0 <= j < count]
+
+    towards, closing_x = steps(2)
+    away, closing_y = steps(-2)
     swap = [(i, i ^ 1) for i in range(count)]
-    got_x = send(payload, towards)
-    got_s = send(payload, swap)
-    got_y = send(payload, away)
-    got_f = send(got_x, swap)
+    closing = dict(closing_x + closing_y)
+    closing = [(i, closing.get(i, i ^ 1)) for i in range(count)]
+    index = lax.axis_index("curve")
+    got_w = lax.ppermute(payload, "curve", closing)
+    got_x = lax.ppermute(payload, "curve", towards)
+    got_y = lax.ppermute(payload, "curve", away)
+    shared = jnp.where((index == 1) | (index == count - 2), got_w, got_x)
+    got_f = lax.ppermute(shared, "curve", swap)
+    cost = pl.CostEstimate(flops=10**9, bytes_accessed=10**6, transcendentals=0)
     hi, lo = pl.pallas_call(
         functools.partial(matrix_kernel, plan),
-        out_shape=(jax.ShapeDtypeStruct((5, cells, cells), BF16),) * 2,
-        in_specs=[vmem] * 3,
-        out_specs=(vmem, vmem),
+        out_shape=(pltpu.VMEM((5, cells, cells), BF16),) * 2,
+        in_specs=[VMEM] * 3,
+        out_specs=(VMEM, VMEM),
         scratch_shapes=[pltpu.VMEM((cells, LANES), F32)],
-        cost_estimate=pl.CostEstimate(flops=2 * 10**9, bytes_accessed=2 * 10**6, transcendentals=0),
+        cost_estimate=cost,
+        compiler_params=GRANT,
         name="matrix",
-    )(src, fr, mo)
+    )(*near(*pieces))
+    acc, hot = pl.pallas_call(
+        functools.partial(first_kernel, plan, count),
+        out_shape=(masses_t, pltpu.VMEM((4, elements, slots), BF16)),
+        in_specs=[VMEM, SMEM] + [VMEM] * 3,
+        out_specs=(VMEM, VMEM),
+        cost_estimate=cost,
+        compiler_params=GRANT,
+        name="first",
+    )(send_ids, send_counts, *near(payload, hi, lo))
+    weights = own_w
+    for names, blocks in (("wx", (got_w, got_x)), ("f", (got_f,))):
+        acc, weights = pl.pallas_call(
+            functools.partial(next_kernel, plan, count, names),
+            out_shape=(masses_t, weights_t),
+            in_specs=[VMEM] * (5 + len(names)),
+            out_specs=(VMEM, VMEM),
+            cost_estimate=cost,
+            compiler_params=GRANT,
+        )(*near(acc, weights, hot, *blocks, hi, lo))
     return pl.pallas_call(
-        functools.partial(final_kernel, plan),
+        functools.partial(last_kernel, plan, count, "y"),
         out_shape=jax.ShapeDtypeStruct((cells, width), F32),
-        in_specs=[vmem, smem] + [vmem] * 8,
-        out_specs=vmem,
-        scratch_shapes=[pltpu.VMEM((plan.tiles, cells, LANES), F32)],
-        name="final",
-    )(send_ids, send_counts, own_w, payload, got_x, got_s, got_y, got_f, hi, lo)
+        in_specs=[VMEM] * 7,
+        out_specs=VMEM,
+        scratch_shapes=[work_t],
+        compiler_params=GRANT,
+        name="last",
+    )(*near(acc, weights, hot, payload, got_y, hi, lo))
 
 
 def solution(mesh):

time: 29 us -> 26.9 us (0.928)
  the two profiles are of different devices: /device:TPU:5 before, /device:TPU:0 now
where the time goes in v2:
time: 26.9 us; the launch traced here: 26.7 us
  waiting for transfers between devices  9.38 us (35%)
  Pallas kernels  9 us (33%)
  starting transfers between devices  8.17 us (30%)
    ppermute x1, starting transfers between devices, local(): got_w = lax.ppermute(payload, 'curve', closing)  6.07 us
    ppermute x1, waiting for transfers between devices, local(): got_x = lax.ppermute(payload, 'curve', towards)  5.26 us
    ppermute x1, waiting for transfers between devices, local(): got_w = lax.ppermute(payload, 'curve', closing)  4.11 us
    pallas_call x1, Pallas kernels, local(): pl.pallas_call(functools.partial(matrix_kernel, plan), out_shape=(pltpu.V...  2.68 us
    pallas_call x2, Pallas kernels, local(): pl.pallas_call(functools.partial(next_kernel, plan, count, names), out_sh...  2.37 us
    ppermute x1, starting transfers between devices, local(): got_y = lax.ppermute(payload, 'curve', away)  2.02 us
    pallas_call x1, Pallas kernels, local(): pl.pallas_call(functools.partial(last_kernel, plan, count, 'y'), out_shap...  1.52 us
    pallas_call x1, Pallas kernels, local(): pl.pallas_call(functools.partial(pack_kernel, plan), out_shape=(pltpu.VME...  1.44 us
  transfers between devices with their start and end apart: 4, of which 2 were waited for; matrix products, arithmetic and copies ran while one was open for 0% of the time, Pallas kernels for 23%

profile of v2, /device:TPU:0, one launch (start us, length us, event | category | flops | bytes accessed | tf_op | source)
XLA Modules:
  0.0 26.7 jit_solution(750296094880353249)
XLA Ops:
  0.0 1.4 %pack.1 = (f32[488,128]{1,0:T(8,128)S(1)}, f32[32,128]{1,0:T(8,128)S(1)}, s32[4,288]{1,0:T(4,128)S(1)}, f32[4,288]{1,0:T(4,128)S(1)}, f32[2,4,288]{2,1,0:T(4,128)S(1)}) custom-call(f32[288,200]{1,0:T(8,128)} %q_hbm.1, s32[4,288]{1,0:T(4,128)} %bitcast.4, f32[4,288]{1,0:T(4,128)} %bitcast.5, f32[2,4,288]{2,1,0:T(4,128)} %bitcast.3, s32[4,32]{1,0:T(4,128)} %ids_ref.1, ...), custom_call_target="tpu_custom_call" | custom-call | tf_op jit(solution)/shard_map/pack/pallas_call | solution.py:359
  1.4 6.1 %collective-permute-start = (f32[488,128]{1,0:T(8,128)S(1)}, f32[488,128]{1,0:T(8,128)S(1)}, u32[]{:S(2)}, u32[]{:S(2)}) collective-permute-start(f32[488,128]{1,0:T(8,128)S(1)} %get-tuple-element.18.own_ref), channel_id=1, source_target_pairs={{0,14},{1,15},{2,3},{3,2},{4,5},{5,4},{6,7},{7,6},{8,9},{9,8},{10,... | collective-permute-start | bytes 749576 | tf_op jit(solution)/shard_map/ppermute | solution.py:392
  7.5 0.0 collective-permute-start.1
  7.5 2.0 %collective-permute-start.3 = (f32[488,128]{1,0:T(8,128)S(1)}, f32[488,128]{1,0:T(8,128)S(1)}, u32[]{:S(2)}, u32[]{:S(2)}) collective-permute-start(f32[488,128]{1,0:T(8,128)S(1)} %get-tuple-element.18.own_ref), channel_id=1, source_target_pairs={{0,2},{1,0},{2,4},{3,1},{4,6},{5,3},{6,8},{7,5},{8,10},{9,7},{10,1... | collective-permute-start | bytes 749576 | tf_op jit(solution)/shard_map/ppermute | solution.py:394
  9.5 4.1 %collective-permute-done.refs_0_ = f32[488,128]{1,0:T(8,128)S(1)} collective-permute-done((f32[488,128]{1,0:T(8,128)S(1)}, f32[488,128]{1,0:T(8,128)S(1)}, u32[]{:S(2)}, u32[]{:S(2)}) %collective-permute-start) | collective-permute-done | bytes 249888 | tf_op jit(solution)/shard_map/ppermute | solution.py:392
  13.7 5.3 %collective-permute-done.1.refs_1_ = f32[488,128]{1,0:T(8,128)S(1)} collective-permute-done((f32[488,128]{1,0:T(8,128)S(1)}, f32[488,128]{1,0:T(8,128)S(1)}, u32[]{:S(2)}, u32[]{:S(2)}) %collective-permute-start.1) | collective-permute-done | bytes 249888 | tf_op jit(solution)/shard_map/ppermute | solution.py:393
  19.0 0.1 collective-permute-start.2
  19.0 0.0 copy-start
  19.0 0.0 copy-start.1
  19.1 2.7 %matrix.1 = (bf16[5,288,288]{2,1,0:T(8,128)(2,1)S(1)}, bf16[5,288,288]{2,1,0:T(8,128)(2,1)S(1)}) custom-call(s32[4,288]{1,0:T(4,128)S(1)} %get-tuple-element.19.src_ref, f32[4,288]{1,0:T(4,128)S(1)} %get-tuple-element.20.fr_ref, f32[2,4,288]{2,1,0:T(4,128)S(1)} %get-tuple-element.21.mo_ref), custom_call_target="tpu_custom_call" | custom-call | flops 1000000000 | bytes 1000000 | tf_op jit(solution)/shard_map/matrix/pallas_call | solution.py:398
  21.7 0.0 copy-done
  21.7 0.0 copy-done.1
  21.8 1.0 %first.1 = (f32[288,256]{1,0:T(8,128)S(1)}, bf16[4,32,32]{2,1,0:T(8,128)(2,1)S(1)}) custom-call(s32[4,32]{1,0:T(4,128)S(1)} %copy-done, s32[4]{0:T(128)S(1)} %copy-done.1, f32[488,128]{1,0:T(8,128)S(1)} %get-tuple-element.18.own_ref, bf16[5,288,288]{2,1,0:T(8,128)(2,1)S(1)} %get-tuple-element.22.hi_ref.refs_2_.refs_1_, ...), custom_call_target="tpu_custom_call" | custom-call | flops 1000000000 | bytes 1000000 | tf_op jit(solution)/shard_map/first/pallas_call | solution.py:408
  22.8 1.6 %shard_map.64 = (f32[288,256]{1,0:T(8,128)S(1)}, f32[32,128]{1,0:T(8,128)S(1)}) custom-call(f32[288,256]{1,0:T(8,128)S(1)} %get-tuple-element.24.in_acc_ref, f32[32,128]{1,0:T(8,128)S(1)} %get-tuple-element.25.in_w_ref, bf16[4,32,32]{2,1,0:T(8,128)(2,1)S(1)} %get-tuple-element.26.hot_ref, f32[488,128]{1,0:T(8,128)S(1)} %collective-permute-done.refs_0_, ...), custom_call_target="tpu_custom_call" | custom-call | flops 1000000000 | bytes 1000000 | tf_op jit(solution)/shard_map/pallas_call | solution.py:419
  24.4 0.0 collective-permute-done.2.refs_0_
  24.4 0.8 %shard_map.65 = (f32[288,256]{1,0:T(8,128)S(1)}, f32[32,128]{1,0:T(8,128)S(1)}) custom-call(f32[288,256]{1,0:T(8,128)S(1)} %get-tuple-element.27.in_acc_ref, f32[32,128]{1,0:T(8,128)S(1)} %get-tuple-element.28.in_w_ref, bf16[4,32,32]{2,1,0:T(8,128)(2,1)S(1)} %get-tuple-element.26.hot_ref, f32[488,128]{1,0:T(8,128)S(1)} %collective-permute-done.2.refs_0_, ...), custom_call_target="tpu_custom_call" | custom-call | flops 1000000000 | bytes 1000000 | tf_op jit(solution)/shard_map/pallas_call | solution.py:419
  25.2 0.0 collective-permute-done.3.ref
  25.2 1.5 %last.1 = f32[288,200]{1,0:T(8,128)} custom-call(f32[288,256]{1,0:T(8,128)S(1)} %get-tuple-element.29.acc_ref, f32[32,128]{1,0:T(8,128)S(1)} %get-tuple-element.30.in_w_ref, bf16[4,32,32]{2,1,0:T(8,128)(2,1)S(1)} %get-tuple-element.26.hot_ref, f32[488,128]{1,0:T(8,128)S(1)} %get-tuple-element.18.own_ref, f32[488,128]{1,0:T(8,128)S(1)} %collective-permute-done.3.ref, ...), custom_call_target="tpu_custom_call" | custom-call | tf_op jit(solution)/shard_map/last/pallas_call | solution.py:427
  (1 shorter events, 0.0 us)
Async XLA Ops:
  1.4 12.2 %collective-permute-start = (f32[488,128]{1,0:T(8,128)S(1)}, f32[488,128]{1,0:T(8,128)S(1)}, u32[]{:S(2)}, u32[]{:S(2)}) collective-permute-start(f32[488,128]{1,0:T(8,128)S(1)} %get-tuple-element.18.own_ref), channel_id=1, source_target_pairs={{0,14},{1,15},{2,3},{3,2},{4,5},{5,4},{6,7},{7,6},{8,9},{9,8},{10,... | collective-permute-start | bytes 749576 | tf_op jit(solution)/shard_map/ppermute | solution.py:392
  7.5 11.4 %collective-permute-start.1 = (f32[488,128]{1,0:T(8,128)S(1)}, f32[488,128]{1,0:T(8,128)S(1)}, u32[]{:S(2)}, u32[]{:S(2)}) collective-permute-start(f32[488,128]{1,0:T(8,128)S(1)} %get-tuple-element.18.own_ref), channel_id=1, source_target_pairs={{0,1},{1,3},{2,0},{3,5},{4,2},{5,7},{6,4},{7,9},{8,6},{9,11},{10,8... | collective-permute-start | bytes 749576 | tf_op jit(solution)/shard_map/ppermute | solution.py:393
  7.5 17.6 %collective-permute-start.3 = (f32[488,128]{1,0:T(8,128)S(1)}, f32[488,128]{1,0:T(8,128)S(1)}, u32[]{:S(2)}, u32[]{:S(2)}) collective-permute-start(f32[488,128]{1,0:T(8,128)S(1)} %get-tuple-element.18.own_ref), channel_id=1, source_target_pairs={{0,2},{1,0},{2,4},{3,1},{4,6},{5,3},{6,8},{7,5},{8,10},{9,7},{10,1... | collective-permute-start | bytes 749576 | tf_op jit(solution)/shard_map/ppermute | solution.py:394
  19.0 5.4 %collective-permute-start.2 = (f32[488,128]{1,0:T(8,128)S(1)}, f32[488,128]{1,0:T(8,128)S(1)}, u32[]{:S(2)}, u32[]{:S(2)}) collective-permute-start(f32[488,128]{1,0:T(8,128)S(1)} %broadcast_select_fusion), channel_id=1, source_target_pairs={{0,1},{1,0},{2,3},{3,2},{4,5},{5,4},{6,7},{7,6},{8,9},{9,8},{10,11... | collective-permute-start | bytes 749576 | tf_op jit(solution)/shard_map/ppermute | solution.py:396
  19.0 2.7 %copy-start = (s32[4,32]{1,0:T(4,128)S(1)}, s32[4,32]{1,0:T(4,128)}, u32[]{:S(2)}) copy-start(s32[4,32]{1,0:T(4,128)} %ids_ref.1) | copy-start | bytes 1540
  19.0 2.7 %copy-start.1 = (s32[4]{0:T(128)S(1)}, s32[4]{0:T(128)}, u32[]{:S(2)}) copy-start(s32[4]{0:T(128)} %cnt_ref.1) | copy-start | bytes 52

commit v3 on v2

v3 whole, which is shorter than its diff:
```python
import functools

import jax
import jax.numpy as jnp
from jax import lax
from jax.experimental import pallas as pl
from jax.experimental.pallas import tpu as pltpu
from jax.sharding import PartitionSpec as P


LANES = 128
F32 = jnp.float32
BF16 = jnp.bfloat16
GROUP = 28


def round8(n):
    return -(-n // 8) * 8


class Plan:
    def __init__(self, cells, width, elements, slots):
        self.cells, self.width, self.elements, self.slots = cells, width, elements, slots
        self.full = width // LANES
        rest = width % LANES
        self.rest = rest
        self.parts = []
        row = self.full * cells
        lane, size = 0, LANES // 2
        self.table = None
        while rest:
            if rest >= size:
                height = round8(-(-cells * size // LANES))
                if rest == size and height <= slots and -(-cells // slots) * size + 2 * GROUP <= LANES:
                    height, self.table, self.base = slots, row, -(-cells // slots) * size
                self.parts.append((lane, size, height, row))
                row += height
                lane += size
                rest -= size
            size //= 2
        if self.table is None:
            self.table, self.base = row, 0
            row += slots
        self.rows = row
        self.tiles = self.full + (1 if self.parts else 0)
        self.lanes = self.tiles * LANES

    def pack(self, tile_rows, outs):
        cells = self.cells
        lanes = lax.broadcasted_iota(jnp.int32, (1, LANES), 1)
        for t in range(self.full):
            tile = tile_rows(t)
            for out, _ in outs:
                out[t * cells:(t + 1) * cells, :] = tile
        if self.parts:
            last = tile_rows(self.full)
        for lane, size, height, first in self.parts:
            total = None
            for g in range(-(-cells // height)):
                count = min(height, cells - g * height)
                piece = last[g * height:g * height + count]
                shift = (g * size - lane) % LANES
                if shift:
                    piece = pltpu.roll(piece, shift, 1)
                if count < height:
                    piece = jnp.concatenate([piece, jnp.zeros((height - count, LANES), F32)], axis=0)
                total = piece if total is None else jnp.where(lanes >= g * size, piece, total)
            for out, table in outs:
                both = jnp.where(lanes >= self.base, table, total) if first == self.table else total
                out[first:first + height, :] = both
        if all(first != self.table for _, _, _, first in self.parts):
            for out, table in outs:
                out[self.table:self.rows, :] = table

    def unpack(self, ref):
        cells = self.cells
        tiles = [ref[t * cells:(t + 1) * cells, :] for t in range(self.full)]
        lanes = lax.broadcasted_iota(jnp.int32, (1, LANES), 1)
        if self.parts:
            last = None
            for lane, size, height, first in self.parts:
                block = ref[first:first + height, :]
                pieces = []
                for g in range(-(-cells // height)):
                    shift = (lane - g * size) % LANES
                    piece = pltpu.roll(block, shift, 1) if shift else block
                    pieces.append(piece[:min(height, cells - g * height)])
                piece = jnp.concatenate(pieces, axis=0)
                last = piece if last is None else jnp.where(lanes >= lane, piece, last)
            tiles.append(last)
        return jnp.concatenate(tiles, axis=1)


def split(x):
    high = x.astype(BF16)
    return high, (x - high.astype(F32)).astype(BF16)


def dot(a, b):
    return jnp.dot(a, b, preferred_element_type=F32)


def element_and_place(src):
    elem = ((src.astype(F32) + 0.5) * (1.0 / 9.0)).astype(jnp.int32)
    return elem, src - 9 * elem


def sent_list(name, count):
    index = lax.axis_index("curve")
    odd = lax.rem(index, 2) == 1
    end = (index == 0) | (index == count - 1)
    beside = (index == 1) | (index == count - 2)
    swap = jnp.where(odd, 2, 0)
    near = jnp.where(odd, 1, 3)
    far = jnp.where(odd, 3, 1)
    if name == "f":
        return jnp.where(odd, 0, 2)
    if name == "w":
        return jnp.where(end, near, jnp.where(beside, far, swap))
    if name == "x":
        return jnp.where(end, swap, near)
    return jnp.where(beside, swap, far)


def table_block(plan, tab_ref, name, count):
    at = plan.elements + plan.slots * lax.rem(sent_list(name, count) + 2, 4)
    return tab_ref[pl.ds(pl.multiple_of(at, 8), plan.slots), :]


def table_for(plan, tab_ref, name, count):
    lanes = lax.broadcasted_iota(jnp.int32, (1, LANES), 1)
    one = table_block(plan, tab_ref, name, count)
    one = pltpu.roll(one, plan.base, 1) if plan.base else one
    two = pltpu.roll(table_block(plan, tab_ref, "f", count), plan.base + GROUP, 1)
    return jnp.where(lanes >= plan.base + GROUP, two, one)


def pack_kernel(plan, count, q_hbm, src_hbm, fr_hbm, mo_hbm, ids_hbm, cnt_hbm,
                x_ref, w_ref, tab_ref, hot_ref, src_ref, fr_ref, mo_ref,
                q_ref, ids_ref, cnt_ref, t_ref, sems):
    E = plan.elements
    copies = [
        pltpu.make_async_copy(a, b, sems.at[n])
        for n, (a, b) in enumerate((
            (src_hbm, src_ref), (fr_hbm, fr_ref), (mo_hbm, mo_ref),
            (cnt_hbm, cnt_ref), (ids_hbm, ids_ref), (q_hbm, q_ref),
        ))
    ]
    for copy in copies:
        copy.start()
    for copy in copies[:5]:
        copy.wait()
    weights_table(plan, src_ref, fr_ref, mo_ref, ids_ref, cnt_ref, tab_ref)
    copies[5].wait()
    for t in range(plan.full):
        t_ref[t] = q_ref[:, t * LANES:(t + 1) * LANES]
    if plan.rest:
        t_ref[plan.full, :, 0:plan.rest] = q_ref[:, plan.full * LANES:plan.width]

    def tile_rows(t):
        return jnp.concatenate([t_ref[t, pl.ds(p, E, stride=9), :] for p in range(9)], axis=0)

    tables = [table_for(plan, tab_ref, name, count) for name in "xw"]
    plan.pack(tile_rows, ((x_ref, tables[0]), (w_ref, tables[1])))
    for n, name in enumerate("wxyf"):
        hot_ref[n] = live_slots(plan, my_list(name, count), ids_ref, cnt_ref)


def weights_table(plan, src_ref, fr_ref, mo_ref, ids_ref, cnt_ref, tab_ref):
    cells, E, S = plan.cells, plan.elements, plan.slots
    elem, place = element_and_place(src_ref[...])
    fr = fr_ref[...]
    wx = fr * mo_ref[0]
    wy = fr * mo_ref[1]
    total = E + 4 * S
    erow = lax.broadcasted_iota(jnp.int32, (total, cells), 0)
    urow = lax.broadcasted_iota(jnp.int32, (32, cells), 0)
    uplace = urow - jnp.where(urow < 9, 0, jnp.where(urow < 18, 9, 18))
    acc = None
    for k in range(src_ref.shape[0]):
        hot = jnp.where(erow == elem[k:k + 1, :], 1.0, 0.0).astype(BF16)
        value = jnp.where(urow < 9, fr[k:k + 1, :], jnp.where(urow < 18, wx[k:k + 1, :], wy[k:k + 1, :]))
        value = jnp.where(uplace == place[k:k + 1, :], value, 0.0)
        high, low = split(value)
        both = jnp.concatenate([high, low, jnp.zeros((64, cells), BF16)], axis=0)
        got = lax.dot_general(hot, both, (((1,), (1,)), ((), ())), preferred_element_type=F32)
        acc = got if acc is None else acc + got
    acc = acc + pltpu.roll(acc, LANES - 32, 1)
    tab_ref[0:E, :] = acc[0:E]
    lane = lax.broadcasted_iota(jnp.int32, (1, LANES), 1)
    diag = lax.broadcasted_iota(jnp.int32, (S, S), 0) == lax.broadcasted_iota(jnp.int32, (S, S), 1)
    slot = lax.broadcasted_iota(jnp.int32, (1, S), 1)
    for o in range(4):
        sent = (o + 2) % 4
        ids = jnp.where(slot < cnt_ref[sent], ids_ref[sent:sent + 1, :].astype(F32), -1.0)
        column = jnp.sum(jnp.where(diag, ids, 0.0), axis=1, keepdims=True)
        part = acc[E + o * S:E + (o + 1) * S]
        tab_ref[E + o * S:E + (o + 1) * S, :] = jnp.where(lane == GROUP - 1, column, part)


def matrix_kernel(plan, src_ref, fr_ref, mo_ref, mat_ref, col_ref):
    cells, E = plan.cells, plan.elements
    K = src_ref.shape[0]
    elem, place = element_and_place(src_ref[...])
    fr = fr_ref[...]
    wx = fr * mo_ref[0]
    wy = fr * mo_ref[1]
    row = jnp.where(place >= 6, 2, jnp.where(place >= 3, 1, 0))
    r = row.astype(F32)
    c = (place - 3 * row).astype(F32)
    centre = fr + wx * (c - 1.0) + wy * (r - 1.0)
    rows = [
        elem.astype(F32), place.astype(F32), centre,
        wx * (1.0 - 0.5 * c), wx * (-0.5 * c), wy * (1.0 - 0.5 * r), wy * (-0.5 * r),
    ]
    rows = jnp.concatenate(rows + [jnp.zeros((LANES - 7 * K, cells), F32)], axis=0)
    pad = -cells % LANES
    if pad:
        rows = jnp.concatenate([rows, jnp.zeros((LANES, pad), F32)], axis=1)
    col_ref[...] = jnp.transpose(rows, (1, 0))[0:cells]
    step = E
    lane = lax.broadcasted_iota(jnp.int32, (step, LANES), 1)
    per = LANES // E
    lists = mat_ref.shape[0]
    main = 8 * E

    def body(i, carry):
        at = pl.multiple_of(i * step, step)
        cols = col_ref[pl.ds(at, step), :]

        def wide(n, k):
            return jnp.broadcast_to(cols[:, n * K + k:n * K + k + 1], (step, LANES))

        inner = (lane % E).astype(F32)
        for t in range(main // LANES + 1):
            tail = t == main // LANES
            where = jnp.full((step, LANES), 8.0) if tail else (lane // E + per * t).astype(F32)
            sums = [jnp.zeros((step, LANES), F32) for _ in range(lists)]
            for k in range(K):
                d = where - wide(1, k)
                coef = jnp.where(d == 0.0, wide(2, k), 0.0)
                coef = jnp.where(d == 1.0, wide(3, k), coef)
                coef = jnp.where(d == 3.0, wide(5, k), coef)
                if not tail:
                    coef = jnp.where(d == -1.0, wide(4, k), coef)
                    coef = jnp.where(d == -3.0, wide(6, k), coef)
                e = wide(0, k) - inner
                for n in range(lists):
                    sums[n] = sums[n] + jnp.where(e == float(n * E), coef, 0.0)
            for n in range(lists):
                high, low = split(sums[n])
                if tail:
                    both = jnp.where(lane < 2 * E, high.astype(F32), low.astype(F32)).astype(BF16)
                    mat_ref[n, pl.ds(at, step), 2 * main:2 * main + LANES] = both
                else:
                    mat_ref[n, pl.ds(at, step), t * LANES:(t + 1) * LANES] = high
                    mat_ref[n, pl.ds(at, step), main + t * LANES:main + (t + 1) * LANES] = low
        return carry

    lax.fori_loop(0, cells // step, body, 0)


def in_slots(plan, masses, ids):
    E = plan.elements
    high, low = split(masses)
    per = LANES // E
    r = lax.broadcasted_iota(jnp.int32, (LANES, LANES), 0)
    l = lax.broadcasted_iota(jnp.int32, (LANES, LANES), 1)
    many = jnp.concatenate([ids] * per, axis=0)
    hot = jnp.where(((l % E).astype(F32) == many) & (r // E == l // E), 1.0, 0.0).astype(BF16)
    pair = jnp.concatenate([high, low], axis=1)
    pieces = []
    for first in range(0, plan.cells, LANES):
        size = min(LANES, plan.cells - first)
        pieces.append(dot(hot[:size, :size], pair[first:first + size]))
    pair = jnp.concatenate(pieces, axis=0)
    return pair[:, :plan.lanes], pair[:, plan.lanes:]


def product(plan, mat, high, low):
    E = plan.elements
    main = 8 * E
    ends = jnp.concatenate([high[main:], low[main:], high[main:]], axis=0)
    return (
        dot(mat[:, :main], high[:main]) + dot(mat[:, :main], low[:main])
        + dot(mat[:, main:2 * main], high[:main]) + dot(mat[:, 2 * main:2 * main + 3 * E], ends)
    )


def group_table(plan, block, group):
    at = plan.base + GROUP * group
    table = block[plan.table:plan.table + plan.slots, :]
    return pltpu.roll(table, LANES - at, 1) if at else table


def returned_weights(table, hot):
    lane = lax.broadcasted_iota(jnp.int32, table.shape, 1)
    high, low = split(jnp.where(lane < GROUP - 1, table, 0.0))
    return dot(hot, high) + dot(hot, low)


def live_slots(plan, which, ids_ref, cnt_ref):
    E, S = plan.elements, plan.slots
    slot = lax.broadcasted_iota(jnp.int32, (E, S), 1)
    e = lax.broadcasted_iota(jnp.int32, (E, S), 0)
    live = (e == ids_ref[pl.ds(which, 1), :]) & (slot < cnt_ref[which])
    return jnp.where(live, 1.0, 0.0).astype(BF16)


def my_list(name, count):
    index = lax.axis_index("curve")
    odd = lax.rem(index, 2) == 1
    end = (index == 0) | (index == count - 1)
    beside = (index == 1) | (index == count - 2)
    swap = jnp.where(odd, 2, 0)
    near = jnp.where(odd, 3, 1)
    far = jnp.where(odd, 1, 3)
    if name == "f":
        return jnp.where(odd, 0, 2)
    if name == "w":
        return jnp.where(end, far, jnp.where(beside, near, swap))
    if name == "x":
        return jnp.where(beside, swap, near)
    return jnp.where(end, swap, far)


def arrived(plan, name, count, block, hot_ref, mat_ref):
    theirs = lax.rem(my_list(name, count) + 2, 4)
    table = group_table(plan, block, 1 if name == "f" else 0)
    weights = returned_weights(table, hot_ref["wxyf".index(name)])
    masses = plan.unpack(block)
    if name == "y":
        high, low = split(masses)
    else:
        high, low = in_slots(plan, masses, table[:, GROUP - 1:GROUP])
        high, low = high.astype(BF16), low.astype(BF16)
    return product(plan, mat_ref[theirs + 1], high, low), weights


def kept(plan, masses, weights, out_ref):
    E = plan.elements
    for p in range(9):
        w = [jnp.broadcast_to(weights[:, 9 * j + p:9 * j + p + 1], (E, LANES)) for j in range(3)]
        for t in range(plan.tiles):
            def at(i):
                return masses[i * E:(i + 1) * E, t * LANES:(t + 1) * LANES]

            def slope(pos, step):
                if pos == 0:
                    return at(p + step) - at(p)
                if pos == 1:
                    return 0.5 * (at(p + step) - at(p - step))
                return at(p) - at(p - step)

            value = at(p) - (w[0] * at(p) + w[1] * slope(p % 3, 1) + w[2] * slope(p // 3, 3))
            out_ref[t, pl.ds(p, E, stride=9), :] = value


def listed_kernel(plan, count, tab_ref, own_ref, y_ref):
    ids = table_block(plan, tab_ref, "y", count)[:, GROUP - 1:GROUP]
    high, low = in_slots(plan, plan.unpack(own_ref), ids)
    listed = high + low
    plan.pack(lambda t: listed[:, t * LANES:(t + 1) * LANES], ((y_ref, table_for(plan, tab_ref, "y", count)),))


def own_kernel(plan, own_ref, mat_ref, acc_ref):
    acc_ref[...] = product(plan, mat_ref[0], *split(plan.unpack(own_ref)))


def pick_kernel(count, w_ref, x_ref, out_ref):
    index = lax.axis_index("curve")
    beside = (index == 1) | (index == count - 2)
    out_ref[...] = jnp.where(beside, w_ref[...], x_ref[...])


def next_kernel(plan, count, names, in_acc_ref, in_w_ref, hot_ref, mat_ref, *refs):
    blocks, (acc_ref, w_ref) = refs[:len(names)], refs[len(names):]
    acc, weights = in_acc_ref[...], in_w_ref[0:plan.elements, :]
    for name, ref in zip(names, blocks):
        more, extra = arrived(plan, name, count, ref, hot_ref, mat_ref)
        acc, weights = acc + more, weights + extra
    acc_ref[...] = acc
    w_ref[...] = weights


def last_kernel(plan, count, name, acc_ref, in_w_ref, hot_ref, mat_ref, own_ref, ref, out_ref, t_ref):
    more, weights = arrived(plan, name, count, ref, hot_ref, mat_ref)
    inflow = acc_ref[...] + more
    kept(plan, plan.unpack(own_ref), in_w_ref[...] + weights, t_ref)
    for t in range(plan.full):
        out_ref[:, t * LANES:(t + 1) * LANES] = t_ref[t] + inflow[:, t * LANES:(t + 1) * LANES]
    if plan.rest:
        at = plan.full * LANES
        out_ref[:, at:plan.width] = (t_ref[plan.full] + inflow[:, at:at + LANES])[:, :plan.rest]


GRANT = pltpu.CompilerParams(vmem_limit_bytes=8 * 2**20)
VMEM = pl.BlockSpec(memory_space=pltpu.VMEM)
SMEM = pl.BlockSpec(memory_space=pltpu.SMEM)


HBM = pl.BlockSpec(memory_space=pltpu.HBM)


def far(*arrays):
    return [pltpu.with_memory_space_constraint(a, pltpu.HBM) for a in arrays]


def near(*arrays):
    return [pltpu.with_memory_space_constraint(a, pltpu.VMEM) for a in arrays]


def local(tracer_mass, send_ids, send_counts, sources, fractions, moments):
    count = lax.axis_size("curve")
    cells, width = tracer_mass.shape
    slots = send_ids.shape[1]
    elements = cells // 9
    plan = Plan(cells, width, elements, slots)
    src, fr, mo = sources.T, fractions.T, jnp.transpose(moments, (0, 2, 1))
    payload_t = pltpu.VMEM((plan.rows, LANES), F32)
    masses_t = pltpu.VMEM((cells, plan.lanes), F32)
    weights_t = pltpu.VMEM((elements, LANES), F32)
    work_t = pltpu.VMEM((plan.tiles, cells, LANES), F32)
    pay_x, pay_w, table, hot, *pieces = pl.pallas_call(
        functools.partial(pack_kernel, plan, count),
        out_shape=(
            payload_t,
            payload_t,
            pltpu.VMEM((elements + 4 * slots, LANES), F32),
            pltpu.VMEM((4, elements, slots), BF16),
            pltpu.VMEM(src.shape, jnp.int32),
            pltpu.VMEM(fr.shape, F32),
            pltpu.VMEM(mo.shape, F32),
        ),
        in_specs=[HBM] * 6,
        out_specs=(VMEM,) * 7,
        scratch_shapes=[
            pltpu.VMEM(tracer_mass.shape, F32),
            pltpu.VMEM(send_ids.shape, jnp.int32),
            pltpu.SMEM(send_counts.shape, jnp.int32),
            work_t,
            pltpu.SemaphoreType.DMA((6,)),
        ],
        compiler_params=GRANT,
        name="pack",
    )(*far(tracer_mass, src, fr, mo, send_ids, send_counts))

    def steps(by):
        pairs = [(i, i + (by if i % 2 else -by)) for i in range(count)]
        inside = [(i, j if 0 <= j < count else i ^ 1) for i, j in pairs]
        return inside, [(i, j % count) for i, j in pairs if not 0 <= j < count]

    towards, closing_x = steps(2)
    away, closing_y = steps(-2)
    swap = [(i, i ^ 1) for i in range(count)]
    closing = dict(closing_x + closing_y)
    closing = [(i, closing.get(i, i ^ 1)) for i in range(count)]
    got_x = lax.ppermute(pay_x, "curve", towards)
    got_w = lax.ppermute(pay_w, "curve", closing)
    cost = pl.CostEstimate(flops=10**9, bytes_accessed=10**6, transcendentals=0)
    matrix = pl.pallas_call(
        functools.partial(matrix_kernel, plan),
        out_shape=pltpu.VMEM((5, cells, 16 * elements + LANES), BF16),
        in_specs=[VMEM] * 3,
        out_specs=VMEM,
        scratch_shapes=[pltpu.VMEM((cells, LANES), F32)],
        cost_estimate=cost,
        compiler_params=GRANT,
        name="matrix",
    )(*near(*pieces))
    pay_y = pl.pallas_call(
        functools.partial(listed_kernel, plan, count),
        out_shape=payload_t,
        in_specs=[VMEM] * 2,
        out_specs=VMEM,
        cost_estimate=cost,
        compiler_params=GRANT,
        name="listed",
    )(*near(table, pay_x))
    acc = pl.pallas_call(
        functools.partial(own_kernel, plan),
        out_shape=masses_t,
        in_specs=[VMEM] * 2,
        out_specs=VMEM,
        cost_estimate=cost,
        compiler_params=GRANT,
        name="own",
    )(*near(pay_x, matrix))
    got_y = lax.ppermute(pay_y, "curve", away)
    shared = pl.pallas_call(
        functools.partial(pick_kernel, count),
        out_shape=payload_t,
        in_specs=[VMEM] * 2,
        out_specs=VMEM,
        cost_estimate=cost,
        compiler_params=GRANT,
        name="pick",
    )(*near(got_w, got_x))
    got_f = lax.ppermute(shared, "curve", swap)
    weights = table
    for names, blocks in (("wx", (got_w, got_x)), ("f", (got_f,))):
        acc, weights = pl.pallas_call(
            functools.partial(next_kernel, plan, count, names),
            out_shape=(masses_t, weights_t),
            in_specs=[VMEM] * (4 + len(names)),
            out_specs=(VMEM, VMEM),
            input_output_aliases={0: 0},
            cost_estimate=cost,
            compiler_params=GRANT,
        )(*near(acc, weights, hot, matrix, *blocks))
    return pl.pallas_call(
        functools.partial(last_kernel, plan, count, "y"),
        out_shape=jax.ShapeDtypeStruct((cells, width), F32),
        in_specs=[VMEM] * 6,
        out_specs=VMEM,
        scratch_shapes=[work_t],
        compiler_params=GRANT,
        name="last",
    )(*near(acc, weights, hot, matrix, pay_x, got_y))


def solution(mesh):
    placed = (
        P(("groups", "curve"), None),
        P(("groups", "curve"), None),
        P(("groups", "curve")),
        P(("groups", "curve"), None),
        P(("groups", "curve"), None),
        P(None, ("groups", "curve"), None),
    )
    return jax.shard_map(
        local, mesh=mesh, in_specs=placed, out_specs=P(("groups", "curve"), None), check_vma=False
    )
```

time: 26.9 us -> 22.1 us (0.82)
  the two profiles are of different devices: /device:TPU:0 before, /device:TPU:17 now
where the time goes in v3:
time: 22.1 us; the launch traced here: 21.9 us
  Pallas kernels  8.07 us (37%)
  waiting for transfers between devices  6.94 us (31%)
  starting transfers between devices  6.87 us (31%)
    ppermute x1, waiting for transfers between devices, local(): got_x = lax.ppermute(pay_x, 'curve', towards)  6.93 us
    ppermute x1, starting transfers between devices, local(): got_f = lax.ppermute(shared, 'curve', swap)  4.39 us
    pallas_call x1, Pallas kernels, local(): pl.pallas_call(functools.partial(matrix_kernel, plan), out_shape=pltpu.VM...  2.64 us
    pallas_call x2, Pallas kernels, local(): pl.pallas_call(functools.partial(next_kernel, plan, count, names), out_sh...  1.99 us
    pallas_call x1, Pallas kernels, local(): pl.pallas_call(functools.partial(pack_kernel, plan, count), out_shape=(pa...  1.39 us
    ppermute x1, starting transfers between devices, local(): got_x = lax.ppermute(pay_x, 'curve', towards)  1.27 us
    pallas_call x1, Pallas kernels, local(): pl.pallas_call(functools.partial(last_kernel, plan, count, 'y'), out_shap...  1.22 us
    ppermute x1, starting transfers between devices, local(): got_w = lax.ppermute(pay_w, 'curve', closing)  0.84 us
  transfers between devices with their start and end apart: 4, of which 1 were waited for; matrix products, arithmetic and copies ran while one was open for 0% of the time, Pallas kernels for 25%

profile of v3, /device:TPU:17, one launch (start us, length us, event | category | flops | bytes accessed | tf_op | source)
XLA Modules:
  0.0 21.9 jit_solution(16102777237718248711)
XLA Ops:
  0.0 1.4 %pack.1 = (f32[464,128]{1,0:T(8,128)S(1)}, f32[464,128]{1,0:T(8,128)S(1)}, f32[160,128]{1,0:T(8,128)S(1)}, bf16[4,32,32]{2,1,0:T(8,128)(2,1)S(1)}, s32[4,288]{1,...) custom-call(f32[288,200]{1,0:T(8,128)} %q_hbm.1, s32[4,288]{1,0:T(4,128)} %bitcast.4, f32[4,288]{1,0:T(4,128)} %bitcast.5, ...), custom_call_target="tpu_custom_call" | custom-call | tf_op jit(solution)/shard_map/pack/pallas_call | solution.py:424
  1.4 1.3 %collective-permute-start.1 = (f32[464,128]{1,0:T(8,128)S(1)}, f32[464,128]{1,0:T(8,128)S(1)}, u32[]{:S(2)}, u32[]{:S(2)}) collective-permute-start(f32[464,128]{1,0:T(8,128)S(1)} %get-tuple-element.16.own_ref), channel_id=1, source_target_pairs={{0,1},{1,3},{2,0},{3,5},{4,2},{5,7},{6,4},{7,9},{8,6},{9,11},{10,8... | collective-permute-start | bytes 712712 | tf_op jit(solution)/shard_map/ppermute | solution.py:458
  2.7 0.8 %collective-permute-start = (f32[464,128]{1,0:T(8,128)S(1)}, f32[464,128]{1,0:T(8,128)S(1)}, u32[]{:S(2)}, u32[]{:S(2)}) collective-permute-start(f32[464,128]{1,0:T(8,128)S(1)} %get-tuple-element.22), channel_id=1, source_target_pairs={{0,14},{1,15},{2,3},{3,2},{4,5},{5,4},{6,7},{7,6},{8,9},{9,8},{10,... | collective-permute-start | bytes 712712 | tf_op jit(solution)/shard_map/ppermute | solution.py:459
  3.5 0.4 %listed.1 = f32[464,128]{1,0:T(8,128)S(1)} custom-call(f32[160,128]{1,0:T(8,128)S(1)} %get-tuple-element.20.in_w_ref.tab_ref, f32[464,128]{1,0:T(8,128)S(1)} %get-tuple-element.16.own_ref), custom_call_target="tpu_custom_call" | custom-call | flops 1000000000 | bytes 1000000 | tf_op jit(solution)/shard_map/listed/pallas_call | solution.py:471
  3.9 0.4 %collective-permute-start.3 = (f32[464,128]{1,0:T(8,128)S(1)}, f32[464,128]{1,0:T(8,128)S(1)}, u32[]{:S(2)}, u32[]{:S(2)}) collective-permute-start(f32[464,128]{1,0:T(8,128)S(1)} %listed.1), channel_id=1, source_target_pairs={{0,2},{1,0},{2,4},{3,1},{4,6},{5,3},{6,8},{7,5},{8,10},{9,7},{10,1... | collective-permute-start | bytes 712712 | tf_op jit(solution)/shard_map/ppermute | solution.py:489
  4.3 6.9 %collective-permute-done.1.refs_1_.x_ref = f32[464,128]{1,0:T(8,128)S(1)} collective-permute-done((f32[464,128]{1,0:T(8,128)S(1)}, f32[464,128]{1,0:T(8,128)S(1)}, u32[]{:S(2)}, u32[]{:S(2)}) %collective-permute-start.1) | collective-permute-done | bytes 237600 | tf_op jit(solution)/shard_map/ppermute | solution.py:458
  11.2 0.0 collective-permute-done.refs_0_.w_ref
  11.3 4.4 %collective-permute-start.2 = (f32[464,128]{1,0:T(8,128)S(1)}, f32[464,128]{1,0:T(8,128)S(1)}, u32[]{:S(2)}, u32[]{:S(2)}) collective-permute-start(f32[464,128]{1,0:T(8,128)S(1)} %pick.1), channel_id=1, source_target_pairs={{0,1},{1,0},{2,3},{3,2},{4,5},{5,4},{6,7},{7,6},{8,9},{9,8},{10,11... | collective-permute-start | bytes 712712 | tf_op jit(solution)/shard_map/ppermute | solution.py:499
  15.6 2.6 %matrix.1.mat_ref = bf16[5,288,640]{2,1,0:T(8,128)(2,1)S(1)} custom-call(s32[4,288]{1,0:T(4,128)S(1)} %get-tuple-element.17.src_ref, f32[4,288]{1,0:T(4,128)S(1)} %get-tuple-element.18.fr_ref, f32[2,4,288]{2,1,0:T(4,128)S(1)} %get-tuple-element.19.mo_ref), custom_call_target="tpu_custom_call" | custom-call | flops 1000000000 | bytes 1000000 | tf_op jit(solution)/shard_map/matrix/pallas_call | solution.py:461
  18.3 0.4 %own.1.in_acc_ref = f32[288,256]{1,0:T(8,128)S(1)} custom-call(f32[464,128]{1,0:T(8,128)S(1)} %get-tuple-element.16.own_ref, bf16[5,288,640]{2,1,0:T(8,128)(2,1)S(1)} %matrix.1.mat_ref), custom_call_target="tpu_custom_call" | custom-call | flops 1000000000 | bytes 1000000 | tf_op jit(solution)/shard_map/own/pallas_call | solution.py:480
  18.7 1.3 %shard_map.64 = (f32[288,256]{1,0:T(8,128)S(1)}, f32[32,128]{1,0:T(8,128)S(1)}) custom-call(f32[288,256]{1,0:T(8,128)S(1)} %own.1.in_acc_ref, f32[160,128]{1,0:T(8,128)S(1)} %get-tuple-element.20.in_w_ref.tab_ref, bf16[4,32,32]{2,1,0:T(8,128)(2,1)S(1)} %get-tuple-element.21.hot_ref, ...), custom_call_target="tpu_custom_call", output_to_operand_aliasing={{0}: (0, {})} | custom-call | flops 1000000000 | bytes 1000000 | tf_op jit(solution)/shard_map/pallas_call | solution.py:502
  20.1 0.0 collective-permute-done.2.refs_0_
  20.1 0.6 %shard_map.65 = (f32[288,256]{1,0:T(8,128)S(1)}, f32[32,128]{1,0:T(8,128)S(1)}) custom-call(f32[288,256]{1,0:T(8,128)S(1)} %get-tuple-element.23.in_acc_ref, f32[32,128]{1,0:T(8,128)S(1)} %get-tuple-element.24.in_w_ref, bf16[4,32,32]{2,1,0:T(8,128)(2,1)S(1)} %get-tuple-element.21.hot_ref, ...), custom_call_target="tpu_custom_call", output_to_operand_aliasing={{0}: (0, {})} | custom-call | flops 1000000000 | bytes 1000000 | tf_op jit(solution)/shard_map/pallas_call | solution.py:502
  20.7 0.0 collective-permute-done.3.ref
  20.7 1.2 %last.1 = f32[288,200]{1,0:T(8,128)} custom-call(f32[288,256]{1,0:T(8,128)S(1)} %get-tuple-element.25.acc_ref, f32[32,128]{1,0:T(8,128)S(1)} %get-tuple-element.26.in_w_ref, bf16[4,32,32]{2,1,0:T(8,128)(2,1)S(1)} %get-tuple-element.21.hot_ref, bf16[5,288,640]{2,1,0:T(8,128)(2,1)S(1)} %matrix.1.mat_ref, f32[464,128]{1,0:T(8,128)S(1)} %get-tuple-element.16.own_ref, ...), custom_call_target="tpu_custom_call" | custom-call | tf_op jit(solution)/shard_map/last/pallas_call | solution.py:511
  (1 shorter events, 0.0 us)
Async XLA Ops:
  1.4 9.8 %collective-permute-start.1 = (f32[464,128]{1,0:T(8,128)S(1)}, f32[464,128]{1,0:T(8,128)S(1)}, u32[]{:S(2)}, u32[]{:S(2)}) collective-permute-start(f32[464,128]{1,0:T(8,128)S(1)} %get-tuple-element.16.own_ref), channel_id=1, source_target_pairs={{0,1},{1,3},{2,0},{3,5},{4,2},{5,7},{6,4},{7,9},{8,6},{9,11},{10,8... | collective-permute-start | bytes 712712 | tf_op jit(solution)/shard_map/ppermute | solution.py:458
  2.7 8.6 %collective-permute-start = (f32[464,128]{1,0:T(8,128)S(1)}, f32[464,128]{1,0:T(8,128)S(1)}, u32[]{:S(2)}, u32[]{:S(2)}) collective-permute-start(f32[464,128]{1,0:T(8,128)S(1)} %get-tuple-element.22), channel_id=1, source_target_pairs={{0,14},{1,15},{2,3},{3,2},{4,5},{5,4},{6,7},{7,6},{8,9},{9,8},{10,... | collective-permute-start | bytes 712712 | tf_op jit(solution)/shard_map/ppermute | solution.py:459
  3.9 16.8 %collective-permute-start.3 = (f32[464,128]{1,0:T(8,128)S(1)}, f32[464,128]{1,0:T(8,128)S(1)}, u32[]{:S(2)}, u32[]{:S(2)}) collective-permute-start(f32[464,128]{1,0:T(8,128)S(1)} %listed.1), channel_id=1, source_target_pairs={{0,2},{1,0},{2,4},{3,1},{4,6},{5,3},{6,8},{7,5},{8,10},{9,7},{10,1... | collective-permute-start | bytes 712712 | tf_op jit(solution)/shard_map/ppermute | solution.py:489
  11.3 8.8 %collective-permute-start.2 = (f32[464,128]{1,0:T(8,128)S(1)}, f32[464,128]{1,0:T(8,128)S(1)}, u32[]{:S(2)}, u32[]{:S(2)}) collective-permute-start(f32[464,128]{1,0:T(8,128)S(1)} %pick.1), channel_id=1, source_target_pairs={{0,1},{1,0},{2,3},{3,2},{4,5},{5,4},{6,7},{7,6},{8,9},{9,8},{10,11... | collective-permute-start | bytes 712712 | tf_op jit(solution)/shard_map/ppermute | solution.py:499

commit v4 on v3

--- a/solution.py
+++ b/solution.py
@@ -329,7 +329,7 @@
     table = group_table(plan, block, 1 if name == "f" else 0)
     weights = returned_weights(table, hot_ref["wxyf".index(name)])
     masses = plan.unpack(block)
-    if name == "y":
+    if name in "fy":
         high, low = split(masses)
     else:
         high, low = in_slots(plan, masses, table[:, GROUP - 1:GROUP])
@@ -367,31 +367,64 @@
     acc_ref[...] = product(plan, mat_ref[0], *split(plan.unpack(own_ref)))
 
 
-def pick_kernel(count, w_ref, x_ref, out_ref):
+def reorder(plan, ref, out_ref):
+    ids = group_table(plan, ref, 1)[:, GROUP - 1:GROUP]
+    high, low = in_slots(plan, plan.unpack(ref), ids)
+    listed = high + low
+    table = ref[plan.table:plan.table + plan.slots, :]
+    plan.pack(lambda t: listed[:, t * LANES:(t + 1) * LANES], ((out_ref, table),))
+
+
+def shared_kernel(plan, x_ref, out_ref):
+    reorder(plan, x_ref, out_ref)
+
+
+def pick_kernel(plan, count, w_ref, x_ref, out_ref):
     index = lax.axis_index("curve")
     beside = (index == 1) | (index == count - 2)
-    out_ref[...] = jnp.where(beside, w_ref[...], x_ref[...])
-
-
-def next_kernel(plan, count, names, in_acc_ref, in_w_ref, hot_ref, mat_ref, *refs):
-    blocks, (acc_ref, w_ref) = refs[:len(names)], refs[len(names):]
-    acc, weights = in_acc_ref[...], in_w_ref[0:plan.elements, :]
-    for name, ref in zip(names, blocks):
+    pl.when(beside)(lambda: reorder(plan, w_ref, out_ref))
+
+    @pl.when(jnp.logical_not(beside))
+    def _():
+        out_ref[...] = x_ref[...]
+
+
+def all_at_once():
+    return lax.axis_index("curve") == 0
+
+
+def next_kernel(plan, count, name, in_acc_ref, in_w_ref, hot_ref, mat_ref, ref, acc_ref, w_ref):
+    def work_off():
+        acc, weights = in_acc_ref[...], in_w_ref[0:plan.elements, :]
         more, extra = arrived(plan, name, count, ref, hot_ref, mat_ref)
-        acc, weights = acc + more, weights + extra
-    acc_ref[...] = acc
-    w_ref[...] = weights
-
-
-def last_kernel(plan, count, name, acc_ref, in_w_ref, hot_ref, mat_ref, own_ref, ref, out_ref, t_ref):
-    more, weights = arrived(plan, name, count, ref, hot_ref, mat_ref)
-    inflow = acc_ref[...] + more
-    kept(plan, plan.unpack(own_ref), in_w_ref[...] + weights, t_ref)
-    for t in range(plan.full):
-        out_ref[:, t * LANES:(t + 1) * LANES] = t_ref[t] + inflow[:, t * LANES:(t + 1) * LANES]
-    if plan.rest:
-        at = plan.full * LANES
-        out_ref[:, at:plan.width] = (t_ref[plan.full] + inflow[:, at:at + LANES])[:, :plan.rest]
+        acc_ref[...] = acc + more
+        w_ref[...] = weights + extra
+
+    if name != "f":
+        return work_off()
+    pl.when(jnp.logical_not(all_at_once()))(work_off)
+
+    @pl.when(all_at_once())
+    def _():
+        acc_ref[...] = in_acc_ref[...]
+        w_ref[...] = in_w_ref[...]
+
+
+def last_kernel(plan, count, acc_ref, in_w_ref, hot_ref, mat_ref, own_ref, f_ref, y_ref, out_ref, t_ref):
+    def work_off(names):
+        inflow, weights = acc_ref[...], in_w_ref[...]
+        for name in names:
+            more, extra = arrived(plan, name, count, f_ref if name == "f" else y_ref, hot_ref, mat_ref)
+            inflow, weights = inflow + more, weights + extra
+        kept(plan, plan.unpack(own_ref), weights, t_ref)
+        for t in range(plan.full):
+            out_ref[:, t * LANES:(t + 1) * LANES] = t_ref[t] + inflow[:, t * LANES:(t + 1) * LANES]
+        if plan.rest:
+            at = plan.full * LANES
+            out_ref[:, at:plan.width] = (t_ref[plan.full] + inflow[:, at:at + LANES])[:, :plan.rest]
+
+    pl.when(all_at_once())(lambda: work_off("fy"))
+    pl.when(jnp.logical_not(all_at_once()))(lambda: work_off("y"))
 
 
 GRANT = pltpu.CompilerParams(vmem_limit_bytes=8 * 2**20)
@@ -488,35 +521,44 @@
     )(*near(pay_x, matrix))
     got_y = lax.ppermute(pay_y, "curve", away)
     shared = pl.pallas_call(
-        functools.partial(pick_kernel, count),
+        functools.partial(shared_kernel, plan),
+        out_shape=payload_t,
+        in_specs=[VMEM],
+        out_specs=VMEM,
+        cost_estimate=cost,
+        compiler_params=GRANT,
+        name="shared",
+    )(*near(got_x))
+    shared = pl.pallas_call(
+        functools.partial(pick_kernel, plan, count),
         out_shape=payload_t,
         in_specs=[VMEM] * 2,
         out_specs=VMEM,
         cost_estimate=cost,
         compiler_params=GRANT,
         name="pick",
-    )(*near(got_w, got_x))
+    )(*near(got_w, shared))
     got_f = lax.ppermute(shared, "curve", swap)
     weights = table
-    for names, blocks in (("wx", (got_w, got_x)), ("f", (got_f,))):
+    for name, block in (("x", got_x), ("w", got_w), ("f", got_f)):
         acc, weights = pl.pallas_call(
-            functools.partial(next_kernel, plan, count, names),
+            functools.partial(next_kernel, plan, count, name),
             out_shape=(masses_t, weights_t),
-            in_specs=[VMEM] * (4 + len(names)),
+            in_specs=[VMEM] * 5,
             out_specs=(VMEM, VMEM),
             input_output_aliases={0: 0},
             cost_estimate=cost,
             compiler_params=GRANT,
-        )(*near(acc, weights, hot, matrix, *blocks))
+        )(*near(acc, weights, hot, matrix, block))
     return pl.pallas_call(
-        functools.partial(last_kernel, plan, count, "y"),
+        functools.partial(last_kernel, plan, count),
         out_shape=jax.ShapeDtypeStruct((cells, width), F32),
-        in_specs=[VMEM] * 6,
+        in_specs=[VMEM] * 7,
         out_specs=VMEM,
         scratch_shapes=[work_t],
         compiler_params=GRANT,
         name="last",
-    )(*near(acc, weights, hot, matrix, pay_x, got_y))
+    )(*near(acc, weights, hot, matrix, pay_x, got_f, got_y))
 
 
 def solution(mesh):

time: 22.1 us -> 19.7 us (0.89)
  the two profiles are of different devices: /device:TPU:17 before, /device:TPU:9 now
where the time goes in v4:
time: 19.7 us; the launch traced here: 19.5 us
  Pallas kernels  8.24 us (42%)
  starting transfers between devices  6.87 us (35%)
  waiting for transfers between devices  4.29 us (22%)
    ppermute x1, starting transfers between devices, local(): got_f = lax.ppermute(shared, 'curve', swap)  4.38 us
    ppermute x1, waiting for transfers between devices, local(): got_x = lax.ppermute(pay_x, 'curve', towards)  4.28 us
    pallas_call x1, Pallas kernels, local(): pl.pallas_call(functools.partial(matrix_kernel, plan), out_shape=pltpu.VM...  2.64 us
    pallas_call x3, Pallas kernels, local(): pl.pallas_call(functools.partial(next_kernel, plan, count, name), out_sha...  1.71 us
    pallas_call x1, Pallas kernels, local(): pl.pallas_call(functools.partial(pack_kernel, plan, count), out_shape=(pa...  1.39 us
    ppermute x1, starting transfers between devices, local(): got_x = lax.ppermute(pay_x, 'curve', towards)  1.27 us
    pallas_call x1, Pallas kernels, local(): pl.pallas_call(functools.partial(last_kernel, plan, count), out_shape=jax...  1.23 us
    ppermute x1, starting transfers between devices, local(): got_w = lax.ppermute(pay_w, 'curve', closing)  0.84 us
  transfers between devices with their start and end apart: 4, of which 1 were waited for; matrix products, arithmetic and copies ran while one was open for 0% of the time, Pallas kernels for 29%

profile of v4, /device:TPU:9, one launch (start us, length us, event | category | flops | bytes accessed | tf_op | source)
XLA Modules:
  0.0 19.5 jit_solution(2533555775034639485)
XLA Ops:
  0.0 1.4 %pack.1 = (f32[464,128]{1,0:T(8,128)S(1)}, f32[464,128]{1,0:T(8,128)S(1)}, f32[160,128]{1,0:T(8,128)S(1)}, bf16[4,32,32]{2,1,0:T(8,128)(2,1)S(1)}, s32[4,288]{1,...) custom-call(f32[288,200]{1,0:T(8,128)} %q_hbm.1, s32[4,288]{1,0:T(4,128)} %bitcast.4, f32[4,288]{1,0:T(4,128)} %bitcast.5, ...), custom_call_target="tpu_custom_call" | custom-call | tf_op jit(solution)/shard_map/pack/pallas_call | solution.py:457
  1.4 1.3 %collective-permute-start = (f32[464,128]{1,0:T(8,128)S(1)}, f32[464,128]{1,0:T(8,128)S(1)}, u32[]{:S(2)}, u32[]{:S(2)}) collective-permute-start(f32[464,128]{1,0:T(8,128)S(1)} %get-tuple-element.18.own_ref), channel_id=1, source_target_pairs={{0,1},{1,3},{2,0},{3,5},{4,2},{5,7},{6,4},{7,9},{8,6},{9,11},{10,8... | collective-permute-start | bytes 712712 | tf_op jit(solution)/shard_map/ppermute | solution.py:491
  2.7 0.8 %collective-permute-start.1 = (f32[464,128]{1,0:T(8,128)S(1)}, f32[464,128]{1,0:T(8,128)S(1)}, u32[]{:S(2)}, u32[]{:S(2)}) collective-permute-start(f32[464,128]{1,0:T(8,128)S(1)} %get-tuple-element.26), channel_id=1, source_target_pairs={{0,14},{1,15},{2,3},{3,2},{4,5},{5,4},{6,7},{7,6},{8,9},{9,8},{10,... | collective-permute-start | bytes 712712 | tf_op jit(solution)/shard_map/ppermute | solution.py:492
  3.5 0.4 %listed.1 = f32[464,128]{1,0:T(8,128)S(1)} custom-call(f32[160,128]{1,0:T(8,128)S(1)} %get-tuple-element.22.in_w_ref.tab_ref, f32[464,128]{1,0:T(8,128)S(1)} %get-tuple-element.18.own_ref), custom_call_target="tpu_custom_call" | custom-call | flops 1000000000 | bytes 1000000 | tf_op jit(solution)/shard_map/listed/pallas_call | solution.py:504
  3.9 0.4 %collective-permute-start.3 = (f32[464,128]{1,0:T(8,128)S(1)}, f32[464,128]{1,0:T(8,128)S(1)}, u32[]{:S(2)}, u32[]{:S(2)}) collective-permute-start(f32[464,128]{1,0:T(8,128)S(1)} %listed.1), channel_id=1, source_target_pairs={{0,2},{1,0},{2,4},{3,1},{4,6},{5,3},{6,8},{7,5},{8,10},{9,7},{10,1... | collective-permute-start | bytes 712712 | tf_op jit(solution)/shard_map/ppermute | solution.py:522
  4.3 2.6 %matrix.1.mat_ref = bf16[5,288,640]{2,1,0:T(8,128)(2,1)S(1)} custom-call(s32[4,288]{1,0:T(4,128)S(1)} %get-tuple-element.19.src_ref, f32[4,288]{1,0:T(4,128)S(1)} %get-tuple-element.20.fr_ref, f32[2,4,288]{2,1,0:T(4,128)S(1)} %get-tuple-element.21.mo_ref), custom_call_target="tpu_custom_call" | custom-call | flops 1000000000 | bytes 1000000 | tf_op jit(solution)/shard_map/matrix/pallas_call | solution.py:494
  6.9 4.3 %collective-permute-done.ref.x_ref = f32[464,128]{1,0:T(8,128)S(1)} collective-permute-done((f32[464,128]{1,0:T(8,128)S(1)}, f32[464,128]{1,0:T(8,128)S(1)}, u32[]{:S(2)}, u32[]{:S(2)}) %collective-permute-start) | collective-permute-done | bytes 237600 | tf_op jit(solution)/shard_map/ppermute | solution.py:491
  11.2 0.4 %shared.1.x_ref = f32[464,128]{1,0:T(8,128)S(1)} custom-call(f32[464,128]{1,0:T(8,128)S(1)} %collective-permute-done.ref.x_ref), custom_call_target="tpu_custom_call" | custom-call | flops 1000000000 | bytes 1000000 | tf_op jit(solution)/shard_map/shared/pallas_call | solution.py:523
  11.7 0.0 collective-permute-done.1.ref.w_ref
  11.7 4.4 %collective-permute-start.2 = (f32[464,128]{1,0:T(8,128)S(1)}, f32[464,128]{1,0:T(8,128)S(1)}, u32[]{:S(2)}, u32[]{:S(2)}) collective-permute-start(f32[464,128]{1,0:T(8,128)S(1)} %pick.1), channel_id=1, source_target_pairs={{0,1},{1,0},{2,3},{3,2},{4,5},{5,4},{6,7},{7,6},{8,9},{9,8},{10,11... | collective-permute-start | bytes 712712 | tf_op jit(solution)/shard_map/ppermute | solution.py:541
  16.1 0.4 %own.1.in_acc_ref = f32[288,256]{1,0:T(8,128)S(1)} custom-call(f32[464,128]{1,0:T(8,128)S(1)} %get-tuple-element.18.own_ref, bf16[5,288,640]{2,1,0:T(8,128)(2,1)S(1)} %matrix.1.mat_ref), custom_call_target="tpu_custom_call" | custom-call | flops 1000000000 | bytes 1000000 | tf_op jit(solution)/shard_map/own/pallas_call | solution.py:513
  16.5 0.6 %shard_map.64 = (f32[288,256]{1,0:T(8,128)S(1)}, f32[32,128]{1,0:T(8,128)S(1)}) custom-call(f32[288,256]{1,0:T(8,128)S(1)} %own.1.in_acc_ref, f32[160,128]{1,0:T(8,128)S(1)} %get-tuple-element.22.in_w_ref.tab_ref, bf16[4,32,32]{2,1,0:T(8,128)(2,1)S(1)} %get-tuple-element.23.hot_ref, ...), custom_call_target="tpu_custom_call", output_to_operand_aliasing={{0}: (0, {})} | custom-call | flops 1000000000 | bytes 1000000 | tf_op jit(solution)/shard_map/pallas_call | solution.py:544
  17.1 0.6 %shard_map.65 = (f32[288,256]{1,0:T(8,128)S(1)}, f32[32,128]{1,0:T(8,128)S(1)}) custom-call(f32[288,256]{1,0:T(8,128)S(1)} %get-tuple-element.24.in_acc_ref, f32[32,128]{1,0:T(8,128)S(1)} %get-tuple-element.25.in_w_ref, bf16[4,32,32]{2,1,0:T(8,128)(2,1)S(1)} %get-tuple-element.23.hot_ref, ...), custom_call_target="tpu_custom_call", output_to_operand_aliasing={{0}: (0, {})} | custom-call | flops 1000000000 | bytes 1000000 | tf_op jit(solution)/shard_map/pallas_call | solution.py:544
  17.8 0.0 collective-permute-done.2.ref.f_ref
  17.8 0.4 %shard_map.66 = (f32[288,256]{1,0:T(8,128)S(1)}, f32[32,128]{1,0:T(8,128)S(1)}) custom-call(f32[288,256]{1,0:T(8,128)S(1)} %get-tuple-element.27.in_acc_ref, f32[32,128]{1,0:T(8,128)S(1)} %get-tuple-element.28.in_w_ref, bf16[4,32,32]{2,1,0:T(8,128)(2,1)S(1)} %get-tuple-element.23.hot_ref, ...), custom_call_target="tpu_custom_call", output_to_operand_aliasing={{0}: (0, {})} | custom-call | flops 1000000000 | bytes 1000000 | tf_op jit(solution)/shard_map/pallas_call | solution.py:544
  18.2 0.0 collective-permute-done.3.y_ref
  18.3 1.2 %last.1 = f32[288,200]{1,0:T(8,128)} custom-call(f32[288,256]{1,0:T(8,128)S(1)} %get-tuple-element.29.acc_ref, f32[32,128]{1,0:T(8,128)S(1)} %get-tuple-element.30.in_w_ref, bf16[4,32,32]{2,1,0:T(8,128)(2,1)S(1)} %get-tuple-element.23.hot_ref, bf16[5,288,640]{2,1,0:T(8,128)(2,1)S(1)} %matrix.1.mat_ref, f32[464,128]{1,0:T(8,128)S(1)} %get-tuple-element.18.own_ref, ...), custom_call_target="tpu_custom_call" | custom-call | tf_op jit(solution)/shard_map/last/pallas_call | solution.py:553
  (1 shorter events, 0.0 us)
Async XLA Ops:
  1.4 9.8 %collective-permute-start = (f32[464,128]{1,0:T(8,128)S(1)}, f32[464,128]{1,0:T(8,128)S(1)}, u32[]{:S(2)}, u32[]{:S(2)}) collective-permute-start(f32[464,128]{1,0:T(8,128)S(1)} %get-tuple-element.18.own_ref), channel_id=1, source_target_pairs={{0,1},{1,3},{2,0},{3,5},{4,2},{5,7},{6,4},{7,9},{8,6},{9,11},{10,8... | collective-permute-start | bytes 712712 | tf_op jit(solution)/shard_map/ppermute | solution.py:491
  2.7 9.0 %collective-permute-start.1 = (f32[464,128]{1,0:T(8,128)S(1)}, f32[464,128]{1,0:T(8,128)S(1)}, u32[]{:S(2)}, u32[]{:S(2)}) collective-permute-start(f32[464,128]{1,0:T(8,128)S(1)} %get-tuple-element.26), channel_id=1, source_target_pairs={{0,14},{1,15},{2,3},{3,2},{4,5},{5,4},{6,7},{7,6},{8,9},{9,8},{10,... | collective-permute-start | bytes 712712 | tf_op jit(solution)/shard_map/ppermute | solution.py:492
  3.9 14.3 %collective-permute-start.3 = (f32[464,128]{1,0:T(8,128)S(1)}, f32[464,128]{1,0:T(8,128)S(1)}, u32[]{:S(2)}, u32[]{:S(2)}) collective-permute-start(f32[464,128]{1,0:T(8,128)S(1)} %listed.1), channel_id=1, source_target_pairs={{0,2},{1,0},{2,4},{3,1},{4,6},{5,3},{6,8},{7,5},{8,10},{9,7},{10,1... | collective-permute-start | bytes 712712 | tf_op jit(solution)/shard_map/ppermute | solution.py:522
  11.7 6.1 %collective-permute-start.2 = (f32[464,128]{1,0:T(8,128)S(1)}, f32[464,128]{1,0:T(8,128)S(1)}, u32[]{:S(2)}, u32[]{:S(2)}) collective-permute-start(f32[464,128]{1,0:T(8,128)S(1)} %pick.1), channel_id=1, source_target_pairs={{0,1},{1,0},{2,3},{3,2},{4,5},{5,4},{6,7},{7,6},{8,9},{9,8},{10,11... | collective-permute-start | bytes 712712 | tf_op jit(solution)/shard_map/ppermute | solution.py:541

commit v5 on v4

--- a/solution.py
+++ b/solution.py
@@ -393,21 +393,28 @@
     return lax.axis_index("curve") == 0
 
 
-def next_kernel(plan, count, name, in_acc_ref, in_w_ref, hot_ref, mat_ref, ref, acc_ref, w_ref):
-    def work_off():
+def next_kernel(plan, count, name, in_acc_ref, in_w_ref, hot_ref, mat_ref, *refs):
+    acc_ref, w_ref = refs[-2:]
+
+    def work_off(names):
         acc, weights = in_acc_ref[...], in_w_ref[0:plan.elements, :]
-        more, extra = arrived(plan, name, count, ref, hot_ref, mat_ref)
-        acc_ref[...] = acc + more
-        w_ref[...] = weights + extra
-
-    if name != "f":
-        return work_off()
-    pl.when(jnp.logical_not(all_at_once()))(work_off)
+        for each, ref in zip(names, refs):
+            more, extra = arrived(plan, each, count, ref, hot_ref, mat_ref)
+            acc, weights = acc + more, weights + extra
+        acc_ref[...] = acc
+        w_ref[...] = weights
+
+    if name == "w":
+        return work_off("w")
+    pl.when(jnp.logical_not(all_at_once()))(lambda: work_off(name))
 
     @pl.when(all_at_once())
     def _():
-        acc_ref[...] = in_acc_ref[...]
-        w_ref[...] = in_w_ref[...]
+        if name == "x":
+            work_off("xy")
+        else:
+            acc_ref[...] = in_acc_ref[...]
+            w_ref[...] = in_w_ref[...]
 
 
 def last_kernel(plan, count, acc_ref, in_w_ref, hot_ref, mat_ref, own_ref, f_ref, y_ref, out_ref, t_ref):
@@ -423,7 +430,7 @@
             at = plan.full * LANES
             out_ref[:, at:plan.width] = (t_ref[plan.full] + inflow[:, at:at + LANES])[:, :plan.rest]
 
-    pl.when(all_at_once())(lambda: work_off("fy"))
+    pl.when(all_at_once())(lambda: work_off("f"))
     pl.when(jnp.logical_not(all_at_once()))(lambda: work_off("y"))
 
 
@@ -520,6 +527,7 @@
         name="own",
     )(*near(pay_x, matrix))
     got_y = lax.ppermute(pay_y, "curve", away)
+    got_s = lax.ppermute(pay_y, "curve", swap)
     shared = pl.pallas_call(
         functools.partial(shared_kernel, plan),
         out_shape=payload_t,
@@ -540,16 +548,16 @@
     )(*near(got_w, shared))
     got_f = lax.ppermute(shared, "curve", swap)
     weights = table
-    for name, block in (("x", got_x), ("w", got_w), ("f", got_f)):
+    for name, blocks in (("x", (got_x, got_s)), ("w", (got_w,)), ("f", (got_f,))):
         acc, weights = pl.pallas_call(
             functools.partial(next_kernel, plan, count, name),
             out_shape=(masses_t, weights_t),
-            in_specs=[VMEM] * 5,
+            in_specs=[VMEM] * (4 + len(blocks)),
             out_specs=(VMEM, VMEM),
             input_output_aliases={0: 0},
             cost_estimate=cost,
             compiler_params=GRANT,
-        )(*near(acc, weights, hot, matrix, block))
+        )(*near(acc, weights, hot, matrix, *blocks))
     return pl.pallas_call(
         functools.partial(last_kernel, plan, count),
         out_shape=jax.ShapeDtypeStruct((cells, width), F32),

time: 19.7 us -> 19.7 us (level)
  the two profiles are of different devices: /device:TPU:9 before, /device:TPU:17 now
where the time goes in v5:
time: 19.7 us; the launch traced here: 19.5 us
  Pallas kernels  8.26 us (42%)
  starting transfers between devices  7.37 us (37%)
  waiting for transfers between devices  3.78 us (19%)
    ppermute x1, starting transfers between devices, local(): got_f = lax.ppermute(shared, 'curve', swap)  4.38 us
    ppermute x1, waiting for transfers between devices, local(): got_x = lax.ppermute(pay_x, 'curve', towards)  3.77 us
    pallas_call x1, Pallas kernels, local(): pl.pallas_call(functools.partial(matrix_kernel, plan), out_shape=pltpu.VM...  2.64 us
    pallas_call x3, Pallas kernels, local(): pl.pallas_call(functools.partial(next_kernel, plan, count, name), out_sha...  1.73 us
    pallas_call x1, Pallas kernels, local(): pl.pallas_call(functools.partial(pack_kernel, plan, count), out_shape=(pa...  1.4 us
    ppermute x1, starting transfers between devices, local(): got_x = lax.ppermute(pay_x, 'curve', towards)  1.27 us
    pallas_call x1, Pallas kernels, local(): pl.pallas_call(functools.partial(last_kernel, plan, count), out_shape=jax...  1.23 us
    ppermute x1, starting transfers between devices, local(): got_w = lax.ppermute(pay_w, 'curve', closing)  0.84 us
  transfers between devices with their start and end apart: 5, of which 1 were waited for; matrix products, arithmetic and copies ran while one was open for 0% of the time, Pallas kernels for 29%

profile of v5, /device:TPU:17, one launch (start us, length us, event | category | flops | bytes accessed | tf_op | source)
XLA Modules:
  0.0 19.5 jit_solution(6061941865563511526)
XLA Ops:
  0.0 1.4 %pack.1 = (f32[464,128]{1,0:T(8,128)S(1)}, f32[464,128]{1,0:T(8,128)S(1)}, f32[160,128]{1,0:T(8,128)S(1)}, bf16[4,32,32]{2,1,0:T(8,128)(2,1)S(1)}, s32[4,288]{1,...) custom-call(f32[288,200]{1,0:T(8,128)} %q_hbm.1, s32[4,288]{1,0:T(4,128)} %bitcast.4, f32[4,288]{1,0:T(4,128)} %bitcast.5, ...), custom_call_target="tpu_custom_call" | custom-call | tf_op jit(solution)/shard_map/pack/pallas_call | solution.py:464
  1.4 1.3 %collective-permute-start = (f32[464,128]{1,0:T(8,128)S(1)}, f32[464,128]{1,0:T(8,128)S(1)}, u32[]{:S(2)}, u32[]{:S(2)}) collective-permute-start(f32[464,128]{1,0:T(8,128)S(1)} %get-tuple-element.18.own_ref), channel_id=1, source_target_pairs={{0,1},{1,3},{2,0},{3,5},{4,2},{5,7},{6,4},{7,9},{8,6},{9,11},{10,8... | collective-permute-start | bytes 712712 | tf_op jit(solution)/shard_map/ppermute | solution.py:498
  2.7 0.8 %collective-permute-start.2 = (f32[464,128]{1,0:T(8,128)S(1)}, f32[464,128]{1,0:T(8,128)S(1)}, u32[]{:S(2)}, u32[]{:S(2)}) collective-permute-start(f32[464,128]{1,0:T(8,128)S(1)} %get-tuple-element.26), channel_id=1, source_target_pairs={{0,14},{1,15},{2,3},{3,2},{4,5},{5,4},{6,7},{7,6},{8,9},{9,8},{10,... | collective-permute-start | bytes 712712 | tf_op jit(solution)/shard_map/ppermute | solution.py:499
  3.5 0.4 %listed.1 = f32[464,128]{1,0:T(8,128)S(1)} custom-call(f32[160,128]{1,0:T(8,128)S(1)} %get-tuple-element.22.tab_ref.in_w_ref, f32[464,128]{1,0:T(8,128)S(1)} %get-tuple-element.18.own_ref), custom_call_target="tpu_custom_call" | custom-call | flops 1000000000 | bytes 1000000 | tf_op jit(solution)/shard_map/listed/pallas_call | solution.py:511
  3.9 0.1 collective-permute-start.1
  4.0 0.8 %collective-permute-start.4 = (f32[464,128]{1,0:T(8,128)S(1)}, f32[464,128]{1,0:T(8,128)S(1)}, u32[]{:S(2)}, u32[]{:S(2)}) collective-permute-start(f32[464,128]{1,0:T(8,128)S(1)} %listed.1), channel_id=1, source_target_pairs={{0,2},{1,0},{2,4},{3,1},{4,6},{5,3},{6,8},{7,5},{8,10},{9,7},{10,1... | collective-permute-start | bytes 712712 | tf_op jit(solution)/shard_map/ppermute | solution.py:529
  4.8 2.6 %matrix.1.mat_ref = bf16[5,288,640]{2,1,0:T(8,128)(2,1)S(1)} custom-call(s32[4,288]{1,0:T(4,128)S(1)} %get-tuple-element.19.src_ref, f32[4,288]{1,0:T(4,128)S(1)} %get-tuple-element.20.fr_ref, f32[2,4,288]{2,1,0:T(4,128)S(1)} %get-tuple-element.21.mo_ref), custom_call_target="tpu_custom_call" | custom-call | flops 1000000000 | bytes 1000000 | tf_op jit(solution)/shard_map/matrix/pallas_call | solution.py:501
  7.5 3.8 %collective-permute-done.refs_0_.x_ref = f32[464,128]{1,0:T(8,128)S(1)} collective-permute-done((f32[464,128]{1,0:T(8,128)S(1)}, f32[464,128]{1,0:T(8,128)S(1)}, u32[]{:S(2)}, u32[]{:S(2)}) %collective-permute-start) | collective-permute-done | bytes 237600 | tf_op jit(solution)/shard_map/ppermute | solution.py:498
  11.2 0.4 %shared.1.x_ref = f32[464,128]{1,0:T(8,128)S(1)} custom-call(f32[464,128]{1,0:T(8,128)S(1)} %collective-permute-done.refs_0_.x_ref), custom_call_target="tpu_custom_call" | custom-call | flops 1000000000 | bytes 1000000 | tf_op jit(solution)/shard_map/shared/pallas_call | solution.py:531
  11.7 0.0 collective-permute-done.2.refs_0_.w_ref
  11.7 4.4 %collective-permute-start.3 = (f32[464,128]{1,0:T(8,128)S(1)}, f32[464,128]{1,0:T(8,128)S(1)}, u32[]{:S(2)}, u32[]{:S(2)}) collective-permute-start(f32[464,128]{1,0:T(8,128)S(1)} %pick.1), channel_id=1, source_target_pairs={{0,1},{1,0},{2,3},{3,2},{4,5},{5,4},{6,7},{7,6},{8,9},{9,8},{10,11... | collective-permute-start | bytes 712712 | tf_op jit(solution)/shard_map/ppermute | solution.py:549
  16.1 0.4 %own.1.in_acc_ref = f32[288,256]{1,0:T(8,128)S(1)} custom-call(f32[464,128]{1,0:T(8,128)S(1)} %get-tuple-element.18.own_ref, bf16[5,288,640]{2,1,0:T(8,128)(2,1)S(1)} %matrix.1.mat_ref), custom_call_target="tpu_custom_call" | custom-call | flops 1000000000 | bytes 1000000 | tf_op jit(solution)/shard_map/own/pallas_call | solution.py:520
  16.5 0.0 collective-permute-done.1.refs_1_
  16.5 0.7 %shard_map.64 = (f32[288,256]{1,0:T(8,128)S(1)}, f32[32,128]{1,0:T(8,128)S(1)}) custom-call(f32[288,256]{1,0:T(8,128)S(1)} %own.1.in_acc_ref, f32[160,128]{1,0:T(8,128)S(1)} %get-tuple-element.22.tab_ref.in_w_ref, bf16[4,32,32]{2,1,0:T(8,128)(2,1)S(1)} %get-tuple-element.23.hot_ref, ...), custom_call_target="tpu_custom_call", output_to_operand_aliasing={{0}: (0, {})} | custom-call | flops 1000000000 | bytes 1000000 | tf_op jit(solution)/shard_map/pallas_call | solution.py:552
  17.2 0.6 %shard_map.65 = (f32[288,256]{1,0:T(8,128)S(1)}, f32[32,128]{1,0:T(8,128)S(1)}) custom-call(f32[288,256]{1,0:T(8,128)S(1)} %get-tuple-element.24.in_acc_ref, f32[32,128]{1,0:T(8,128)S(1)} %get-tuple-element.25.in_w_ref, bf16[4,32,32]{2,1,0:T(8,128)(2,1)S(1)} %get-tuple-element.23.hot_ref, ...), custom_call_target="tpu_custom_call", output_to_operand_aliasing={{0}: (0, {})} | custom-call | flops 1000000000 | bytes 1000000 | tf_op jit(solution)/shard_map/pallas_call | solution.py:552
  17.8 0.0 collective-permute-done.3.refs_0_.f_ref
  17.8 0.4 %shard_map.66 = (f32[288,256]{1,0:T(8,128)S(1)}, f32[32,128]{1,0:T(8,128)S(1)}) custom-call(f32[288,256]{1,0:T(8,128)S(1)} %get-tuple-element.27.in_acc_ref, f32[32,128]{1,0:T(8,128)S(1)} %get-tuple-element.28.in_w_ref, bf16[4,32,32]{2,1,0:T(8,128)(2,1)S(1)} %get-tuple-element.23.hot_ref, ...), custom_call_target="tpu_custom_call", output_to_operand_aliasing={{0}: (0, {})} | custom-call | flops 1000000000 | bytes 1000000 | tf_op jit(solution)/shard_map/pallas_call | solution.py:552
  18.3 0.0 collective-permute-done.4.y_ref
  18.3 1.2 %last.1 = f32[288,200]{1,0:T(8,128)} custom-call(f32[288,256]{1,0:T(8,128)S(1)} %get-tuple-element.29.acc_ref, f32[32,128]{1,0:T(8,128)S(1)} %get-tuple-element.30.in_w_ref, bf16[4,32,32]{2,1,0:T(8,128)(2,1)S(1)} %get-tuple-element.23.hot_ref, bf16[5,288,640]{2,1,0:T(8,128)(2,1)S(1)} %matrix.1.mat_ref, f32[464,128]{1,0:T(8,128)S(1)} %get-tuple-element.18.own_ref, ...), custom_call_target="tpu_custom_call" | custom-call | tf_op jit(solution)/shard_map/last/pallas_call | solution.py:561
  (1 shorter events, 0.0 us)
Async XLA Ops:
  1.4 9.8 %collective-permute-start = (f32[464,128]{1,0:T(8,128)S(1)}, f32[464,128]{1,0:T(8,128)S(1)}, u32[]{:S(2)}, u32[]{:S(2)}) collective-permute-start(f32[464,128]{1,0:T(8,128)S(1)} %get-tuple-element.18.own_ref), channel_id=1, source_target_pairs={{0,1},{1,3},{2,0},{3,5},{4,2},{5,7},{6,4},{7,9},{8,6},{9,11},{10,8... | collective-permute-start | bytes 712712 | tf_op jit(solution)/shard_map/ppermute | solution.py:498
  2.7 9.0 %collective-permute-start.2 = (f32[464,128]{1,0:T(8,128)S(1)}, f32[464,128]{1,0:T(8,128)S(1)}, u32[]{:S(2)}, u32[]{:S(2)}) collective-permute-start(f32[464,128]{1,0:T(8,128)S(1)} %get-tuple-element.26), channel_id=1, source_target_pairs={{0,14},{1,15},{2,3},{3,2},{4,5},{5,4},{6,7},{7,6},{8,9},{9,8},{10,... | collective-permute-start | bytes 712712 | tf_op jit(solution)/shard_map/ppermute | solution.py:499
  3.9 12.6 %collective-permute-start.1 = (f32[464,128]{1,0:T(8,128)S(1)}, f32[464,128]{1,0:T(8,128)S(1)}, u32[]{:S(2)}, u32[]{:S(2)}) collective-permute-start(f32[464,128]{1,0:T(8,128)S(1)} %listed.1), channel_id=1, source_target_pairs={{0,1},{1,0},{2,3},{3,2},{4,5},{5,4},{6,7},{7,6},{8,9},{9,8},{10,11... | collective-permute-start | bytes 712712 | tf_op jit(solution)/shard_map/ppermute | solution.py:530
  4.0 14.3 %collective-permute-start.4 = (f32[464,128]{1,0:T(8,128)S(1)}, f32[464,128]{1,0:T(8,128)S(1)}, u32[]{:S(2)}, u32[]{:S(2)}) collective-permute-start(f32[464,128]{1,0:T(8,128)S(1)} %listed.1), channel_id=1, source_target_pairs={{0,2},{1,0},{2,4},{3,1},{4,6},{5,3},{6,8},{7,5},{8,10},{9,7},{10,1... | collective-permute-start | bytes 712712 | tf_op jit(solution)/shard_map/ppermute | solution.py:529
  11.7 6.1 %collective-permute-start.3 = (f32[464,128]{1,0:T(8,128)S(1)}, f32[464,128]{1,0:T(8,128)S(1)}, u32[]{:S(2)}, u32[]{:S(2)}) collective-permute-start(f32[464,128]{1,0:T(8,128)S(1)} %pick.1), channel_id=1, source_target_pairs={{0,1},{1,0},{2,3},{3,2},{4,5},{5,4},{6,7},{7,6},{8,9},{9,8},{10,11... | collective-permute-start | bytes 712712 | tf_op jit(solution)/shard_map/ppermute | solution.py:549

commit v6 on v4

--- a/solution.py
+++ b/solution.py
@@ -173,18 +173,23 @@
     wx = fr * mo_ref[0]
     wy = fr * mo_ref[1]
     total = E + 4 * S
-    erow = lax.broadcasted_iota(jnp.int32, (total, cells), 0)
-    urow = lax.broadcasted_iota(jnp.int32, (32, cells), 0)
+    pieces = src_ref.shape[0]
+    main = cells // LANES * LANES
+
+    def flat(x):
+        rows = [x[k:k + 1, :main] for k in range(pieces)]
+        return jnp.concatenate(rows + [x[k:k + 1, main:] for k in range(pieces)], axis=1)
+
+    elem, place, fr, wx, wy = (flat(x) for x in (elem, place, fr, wx, wy))
+    many = pieces * cells
+    erow = lax.broadcasted_iota(jnp.int32, (total, many), 0)
+    urow = lax.broadcasted_iota(jnp.int32, (32, many), 0)
     uplace = urow - jnp.where(urow < 9, 0, jnp.where(urow < 18, 9, 18))
-    acc = None
-    for k in range(src_ref.shape[0]):
-        hot = jnp.where(erow == elem[k:k + 1, :], 1.0, 0.0).astype(BF16)
-        value = jnp.where(urow < 9, fr[k:k + 1, :], jnp.where(urow < 18, wx[k:k + 1, :], wy[k:k + 1, :]))
-        value = jnp.where(uplace == place[k:k + 1, :], value, 0.0)
-        high, low = split(value)
-        both = jnp.concatenate([high, low, jnp.zeros((64, cells), BF16)], axis=0)
-        got = lax.dot_general(hot, both, (((1,), (1,)), ((), ())), preferred_element_type=F32)
-        acc = got if acc is None else acc + got
+    hot = jnp.where(erow == elem, 1.0, 0.0).astype(BF16)
+    value = jnp.where(urow < 9, fr, jnp.where(urow < 18, wx, wy))
+    high, low = split(jnp.where(uplace == place, value, 0.0))
+    both = jnp.concatenate([high, low, jnp.zeros((64, many), BF16)], axis=0)
+    acc = lax.dot_general(hot, both, (((1,), (1,)), ((), ())), preferred_element_type=F32)
     acc = acc + pltpu.roll(acc, LANES - 32, 1)
     tab_ref[0:E, :] = acc[0:E]
     lane = lax.broadcasted_iota(jnp.int32, (1, LANES), 1)
@@ -363,8 +368,10 @@
     plan.pack(lambda t: listed[:, t * LANES:(t + 1) * LANES], ((y_ref, table_for(plan, tab_ref, "y", count)),))
 
 
-def own_kernel(plan, own_ref, mat_ref, acc_ref):
-    acc_ref[...] = product(plan, mat_ref[0], *split(plan.unpack(own_ref)))
+def own_kernel(plan, own_ref, mat_ref, acc_ref, masses_ref):
+    masses = plan.unpack(own_ref)
+    masses_ref[...] = masses
+    acc_ref[...] = product(plan, mat_ref[0], *split(masses))
 
 
 def reorder(plan, ref, out_ref):
@@ -416,7 +423,7 @@
         for name in names:
             more, extra = arrived(plan, name, count, f_ref if name == "f" else y_ref, hot_ref, mat_ref)
             inflow, weights = inflow + more, weights + extra
-        kept(plan, plan.unpack(own_ref), weights, t_ref)
+        kept(plan, own_ref[...], weights, t_ref)
         for t in range(plan.full):
             out_ref[:, t * LANES:(t + 1) * LANES] = t_ref[t] + inflow[:, t * LANES:(t + 1) * LANES]
         if plan.rest:
@@ -510,11 +517,11 @@
         compiler_params=GRANT,
         name="listed",
     )(*near(table, pay_x))
-    acc = pl.pallas_call(
+    acc, masses = pl.pallas_call(
         functools.partial(own_kernel, plan),
-        out_shape=masses_t,
+        out_shape=(masses_t, masses_t),
         in_specs=[VMEM] * 2,
-        out_specs=VMEM,
+        out_specs=(VMEM, VMEM),
         cost_estimate=cost,
         compiler_params=GRANT,
         name="own",
@@ -558,7 +565,7 @@
         scratch_shapes=[work_t],
         compiler_params=GRANT,
         name="last",
-    )(*near(acc, weights, hot, matrix, pay_x, got_f, got_y))
+    )(*near(acc, weights, hot, matrix, masses, got_f, got_y))
 
 
 def solution(mesh):

time: 19.7 us -> 19.6 us (level)
  the two profiles are of different devices: /device:TPU:9 before, /device:TPU:13 now
where the time goes in v6:
time: 19.6 us; the launch traced here: 19.5 us
  Pallas kernels  8.2 us (42%)
  starting transfers between devices  6.87 us (35%)
  waiting for transfers between devices  4.29 us (22%)
    ppermute x1, starting transfers between devices, local(): got_f = lax.ppermute(shared, 'curve', swap)  4.38 us
    ppermute x1, waiting for transfers between devices, local(): got_x = lax.ppermute(pay_x, 'curve', towards)  4.28 us
    pallas_call x1, Pallas kernels, local(): pl.pallas_call(functools.partial(matrix_kernel, plan), out_shape=pltpu.VM...  2.64 us
    pallas_call x3, Pallas kernels, local(): pl.pallas_call(functools.partial(next_kernel, plan, count, name), out_sha...  1.71 us
    pallas_call x1, Pallas kernels, local(): pl.pallas_call(functools.partial(pack_kernel, plan, count), out_shape=(pa...  1.38 us
    ppermute x1, starting transfers between devices, local(): got_x = lax.ppermute(pay_x, 'curve', towards)  1.27 us
    pallas_call x1, Pallas kernels, local(): pl.pallas_call(functools.partial(last_kernel, plan, count), out_shape=jax...  1.22 us
    ppermute x1, starting transfers between devices, local(): got_w = lax.ppermute(pay_w, 'curve', closing)  0.84 us
  transfers between devices with their start and end apart: 4, of which 1 were waited for; matrix products, arithmetic and copies ran while one was open for 0% of the time, Pallas kernels for 29%

profile of v6, /device:TPU:13, one launch (start us, length us, event | category | flops | bytes accessed | tf_op | source)
XLA Modules:
  0.0 19.5 jit_solution(17741858950593613761)
XLA Ops:
  0.0 1.4 %pack.1 = (f32[464,128]{1,0:T(8,128)S(1)}, f32[464,128]{1,0:T(8,128)S(1)}, f32[160,128]{1,0:T(8,128)S(1)}, bf16[4,32,32]{2,1,0:T(8,128)(2,1)S(1)}, s32[4,288]{1,...) custom-call(f32[288,200]{1,0:T(8,128)} %q_hbm.1, s32[4,288]{1,0:T(4,128)} %bitcast.4, f32[4,288]{1,0:T(4,128)} %bitcast.5, ...), custom_call_target="tpu_custom_call" | custom-call | tf_op jit(solution)/shard_map/pack/pallas_call | solution.py:464
  1.4 1.3 %collective-permute-start = (f32[464,128]{1,0:T(8,128)S(1)}, f32[464,128]{1,0:T(8,128)S(1)}, u32[]{:S(2)}, u32[]{:S(2)}) collective-permute-start(f32[464,128]{1,0:T(8,128)S(1)} %get-tuple-element.20.own_ref), channel_id=1, source_target_pairs={{0,1},{1,3},{2,0},{3,5},{4,2},{5,7},{6,4},{7,9},{8,6},{9,11},{10,8... | collective-permute-start | bytes 712712 | tf_op jit(solution)/shard_map/ppermute | solution.py:498
  2.7 0.8 %collective-permute-start.1 = (f32[464,128]{1,0:T(8,128)S(1)}, f32[464,128]{1,0:T(8,128)S(1)}, u32[]{:S(2)}, u32[]{:S(2)}) collective-permute-start(f32[464,128]{1,0:T(8,128)S(1)} %get-tuple-element.29), channel_id=1, source_target_pairs={{0,14},{1,15},{2,3},{3,2},{4,5},{5,4},{6,7},{7,6},{8,9},{9,8},{10,... | collective-permute-start | bytes 712712 | tf_op jit(solution)/shard_map/ppermute | solution.py:499
  3.5 0.4 %listed.1 = f32[464,128]{1,0:T(8,128)S(1)} custom-call(f32[160,128]{1,0:T(8,128)S(1)} %get-tuple-element.25.in_w_ref.tab_ref, f32[464,128]{1,0:T(8,128)S(1)} %get-tuple-element.20.own_ref), custom_call_target="tpu_custom_call" | custom-call | flops 1000000000 | bytes 1000000 | tf_op jit(solution)/shard_map/listed/pallas_call | solution.py:511
  3.9 0.4 %collective-permute-start.3 = (f32[464,128]{1,0:T(8,128)S(1)}, f32[464,128]{1,0:T(8,128)S(1)}, u32[]{:S(2)}, u32[]{:S(2)}) collective-permute-start(f32[464,128]{1,0:T(8,128)S(1)} %listed.1), channel_id=1, source_target_pairs={{0,2},{1,0},{2,4},{3,1},{4,6},{5,3},{6,8},{7,5},{8,10},{9,7},{10,1... | collective-permute-start | bytes 712712 | tf_op jit(solution)/shard_map/ppermute | solution.py:529
  4.3 2.6 %matrix.1.mat_ref = bf16[5,288,640]{2,1,0:T(8,128)(2,1)S(1)} custom-call(s32[4,288]{1,0:T(4,128)S(1)} %get-tuple-element.21.src_ref, f32[4,288]{1,0:T(4,128)S(1)} %get-tuple-element.22.fr_ref, f32[2,4,288]{2,1,0:T(4,128)S(1)} %get-tuple-element.23.mo_ref), custom_call_target="tpu_custom_call" | custom-call | flops 1000000000 | bytes 1000000 | tf_op jit(solution)/shard_map/matrix/pallas_call | solution.py:501
  6.9 4.3 %collective-permute-done.ref.x_ref = f32[464,128]{1,0:T(8,128)S(1)} collective-permute-done((f32[464,128]{1,0:T(8,128)S(1)}, f32[464,128]{1,0:T(8,128)S(1)}, u32[]{:S(2)}, u32[]{:S(2)}) %collective-permute-start) | collective-permute-done | bytes 237600 | tf_op jit(solution)/shard_map/ppermute | solution.py:498
  11.2 0.4 %shared.1.x_ref = f32[464,128]{1,0:T(8,128)S(1)} custom-call(f32[464,128]{1,0:T(8,128)S(1)} %collective-permute-done.ref.x_ref), custom_call_target="tpu_custom_call" | custom-call | flops 1000000000 | bytes 1000000 | tf_op jit(solution)/shard_map/shared/pallas_call | solution.py:530
  11.6 0.0 collective-permute-done.1.ref.w_ref
  11.7 4.4 %collective-permute-start.2 = (f32[464,128]{1,0:T(8,128)S(1)}, f32[464,128]{1,0:T(8,128)S(1)}, u32[]{:S(2)}, u32[]{:S(2)}) collective-permute-start(f32[464,128]{1,0:T(8,128)S(1)} %pick.1), channel_id=1, source_target_pairs={{0,1},{1,0},{2,3},{3,2},{4,5},{5,4},{6,7},{7,6},{8,9},{9,8},{10,11... | collective-permute-start | bytes 712712 | tf_op jit(solution)/shard_map/ppermute | solution.py:548
  16.1 0.4 %own.1 = (f32[288,256]{1,0:T(8,128)S(1)}, f32[288,256]{1,0:T(8,128)S(1)}) custom-call(f32[464,128]{1,0:T(8,128)S(1)} %get-tuple-element.20.own_ref, bf16[5,288,640]{2,1,0:T(8,128)(2,1)S(1)} %matrix.1.mat_ref), custom_call_target="tpu_custom_call" | custom-call | flops 1000000000 | bytes 1000000 | tf_op jit(solution)/shard_map/own/pallas_call | solution.py:520
  16.5 0.6 %shard_map.64 = (f32[288,256]{1,0:T(8,128)S(1)}, f32[32,128]{1,0:T(8,128)S(1)}) custom-call(f32[288,256]{1,0:T(8,128)S(1)} %get-tuple-element.24.in_acc_ref, f32[160,128]{1,0:T(8,128)S(1)} %get-tuple-element.25.in_w_ref.tab_ref, bf16[4,32,32]{2,1,0:T(8,128)(2,1)S(1)} %get-tuple-element.26.hot_ref, ...), custom_call_target="tpu_custom_call", output_to_operand_aliasing={{0}: (0, {})} | custom-call | flops 1000000000 | bytes 1000000 | tf_op jit(solution)/shard_map/pallas_call | solution.py:551
  17.1 0.6 %shard_map.65 = (f32[288,256]{1,0:T(8,128)S(1)}, f32[32,128]{1,0:T(8,128)S(1)}) custom-call(f32[288,256]{1,0:T(8,128)S(1)} %get-tuple-element.27.in_acc_ref, f32[32,128]{1,0:T(8,128)S(1)} %get-tuple-element.28.in_w_ref, bf16[4,32,32]{2,1,0:T(8,128)(2,1)S(1)} %get-tuple-element.26.hot_ref, ...), custom_call_target="tpu_custom_call", output_to_operand_aliasing={{0}: (0, {})} | custom-call | flops 1000000000 | bytes 1000000 | tf_op jit(solution)/shard_map/pallas_call | solution.py:551
  17.8 0.0 collective-permute-done.2.ref.f_ref
  17.8 0.4 %shard_map.66 = (f32[288,256]{1,0:T(8,128)S(1)}, f32[32,128]{1,0:T(8,128)S(1)}) custom-call(f32[288,256]{1,0:T(8,128)S(1)} %get-tuple-element.30.in_acc_ref, f32[32,128]{1,0:T(8,128)S(1)} %get-tuple-element.31.in_w_ref, bf16[4,32,32]{2,1,0:T(8,128)(2,1)S(1)} %get-tuple-element.26.hot_ref, ...), custom_call_target="tpu_custom_call", output_to_operand_aliasing={{0}: (0, {})} | custom-call | flops 1000000000 | bytes 1000000 | tf_op jit(solution)/shard_map/pallas_call | solution.py:551
  18.2 0.0 collective-permute-done.3.y_ref
  18.2 1.2 %last.1 = f32[288,200]{1,0:T(8,128)} custom-call(f32[288,256]{1,0:T(8,128)S(1)} %get-tuple-element.32.acc_ref, f32[32,128]{1,0:T(8,128)S(1)} %get-tuple-element.33.in_w_ref, bf16[4,32,32]{2,1,0:T(8,128)(2,1)S(1)} %get-tuple-element.26.hot_ref, bf16[5,288,640]{2,1,0:T(8,128)(2,1)S(1)} %matrix.1.mat_ref, f32[288,256]{1,0:T(8,128)S(1)} %get-tuple-element.34.own_ref, ...), custom_call_target="tpu_custom_call" | custom-call | tf_op jit(solution)/shard_map/last/pallas_call | solution.py:560
  (1 shorter events, 0.0 us)
Async XLA Ops:
  1.4 9.8 %collective-permute-start = (f32[464,128]{1,0:T(8,128)S(1)}, f32[464,128]{1,0:T(8,128)S(1)}, u32[]{:S(2)}, u32[]{:S(2)}) collective-permute-start(f32[464,128]{1,0:T(8,128)S(1)} %get-tuple-element.20.own_ref), channel_id=1, source_target_pairs={{0,1},{1,3},{2,0},{3,5},{4,2},{5,7},{6,4},{7,9},{8,6},{9,11},{10,8... | collective-permute-start | bytes 712712 | tf_op jit(solution)/shard_map/ppermute | solution.py:498
  2.7 9.0 %collective-permute-start.1 = (f32[464,128]{1,0:T(8,128)S(1)}, f32[464,128]{1,0:T(8,128)S(1)}, u32[]{:S(2)}, u32[]{:S(2)}) collective-permute-start(f32[464,128]{1,0:T(8,128)S(1)} %get-tuple-element.29), channel_id=1, source_target_pairs={{0,14},{1,15},{2,3},{3,2},{4,5},{5,4},{6,7},{7,6},{8,9},{9,8},{10,... | collective-permute-start | bytes 712712 | tf_op jit(solution)/shard_map/ppermute | solution.py:499
  3.9 14.3 %collective-permute-start.3 = (f32[464,128]{1,0:T(8,128)S(1)}, f32[464,128]{1,0:T(8,128)S(1)}, u32[]{:S(2)}, u32[]{:S(2)}) collective-permute-start(f32[464,128]{1,0:T(8,128)S(1)} %listed.1), channel_id=1, source_target_pairs={{0,2},{1,0},{2,4},{3,1},{4,6},{5,3},{6,8},{7,5},{8,10},{9,7},{10,1... | collective-permute-start | bytes 712712 | tf_op jit(solution)/shard_map/ppermute | solution.py:529
  11.7 6.1 %collective-permute-start.2 = (f32[464,128]{1,0:T(8,128)S(1)}, f32[464,128]{1,0:T(8,128)S(1)}, u32[]{:S(2)}, u32[]{:S(2)}) collective-permute-start(f32[464,128]{1,0:T(8,128)S(1)} %pick.1), channel_id=1, source_target_pairs={{0,1},{1,0},{2,3},{3,2},{4,5},{5,4},{6,7},{7,6},{8,9},{9,8},{10,11... | collective-permute-start | bytes 712712 | tf_op jit(solution)/shard_map/ppermute | solution.py:548
